TPU v7x, 128 devices: a whole 4x4x4 slice. The times are simulated.
128 devices in a mesh: tm: 32 (over y, z, core), node: 4 (over x).
Axes of the slice: x: 4, y: 4, z: 4, core: 2. Of those that a mesh axis runs over, the one named last changes fastest.
Arguments:
- slice_starts: float32 [32, 32, 16384], P('tm'), may hold values from -1 to 1
- coupling: float32 [32, 16384], replicated, may hold values from 0.03 to 0.25
Outputs:
- node_values: float32 [32, 4, 32, 16384], P('tm', 'node')
- residual_log: float32 [3, 32], replicated
All inputs are finite; a program needn't handle non-finite values.
Results may differ from a plain program's by a relative error of at most 0.0001.
Values sent between devices are 32-bit elements.
A program may use at most 128 MiB of HBM per device.

v0:
```python
import jax
import jax.numpy as jnp
from jax import lax
from jax.sharding import PartitionSpec as P

M = 4
SWEEPS = 3
NEWTON = 2


time_step = 0.5
log_floor = 0.05


def spread(value, axis, root):
    mine = lax.axis_index(axis) == root
    return lax.psum(jnp.where(mine, value, jnp.zeros_like(value)), axis)


def passed_along(value, axis, by):
    size = lax.axis_size(axis)
    pairs = [(i, i + by) for i in range(size) if 0 <= i + by < size]
    return lax.ppermute(value, axis, pairs)


def total_of_pieces(value, axis):
    return lax.all_gather(value, axis).sum(0)


def legendre_gap(point, node_count):
    before = 1.0
    current = point
    for degree in range(1, node_count):
        following = ((2 * degree + 1) * point * current - degree * before) / (degree + 1)
        before = current
        current = following
    return current - before


def collocation(node_count):
    points = []
    samples = 4000
    for sample_index in range(samples - 1):
        lower_end = -1.0 + 2.0 * sample_index / samples
        upper_end = -1.0 + 2.0 * (sample_index + 1) / samples
        lower_value = legendre_gap(lower_end, node_count)
        upper_value = legendre_gap(upper_end, node_count)
        if lower_value * upper_value < 0.0:
            for halving in range(80):
                middle = 0.5 * (lower_end + upper_end)
                middle_value = legendre_gap(middle, node_count)
                if lower_value * middle_value <= 0.0:
                    upper_end = middle
                else:
                    lower_end = middle
                    lower_value = middle_value
            points.append(0.5 * (lower_end + upper_end))
    points.append(1.0)
    node_times = [(point + 1.0) / 2.0 for point in points]
    matrix = [[0.0] * node_count for row_index in range(node_count)]
    for column in range(node_count):
        coeffs = [1.0]
        for other in range(node_count):
            if other != column:
                scale = node_times[column] - node_times[other]
                shifted = [0.0] + coeffs
                scaled = [value * node_times[other] for value in coeffs] + [0.0]
                coeffs = [(shifted[power] - scaled[power]) / scale for power in range(len(shifted))]
        for row_index in range(node_count):
            upper_time = node_times[row_index]
            matrix[row_index][column] = sum(
                (
                    coeffs[power] * upper_time ** (power + 1) / (power + 1)
                    for power in range(len(coeffs))
                )
            )
    return (node_times, matrix)


def operator_term(field_values, coupling):
    right_side = jnp.roll(field_values, -1, axis=-1)
    left_side = jnp.roll(field_values, 1, axis=-1)
    left_coupling = jnp.roll(coupling, 1, axis=-1)
    cubic = field_values * field_values * field_values
    return (
        coupling * (right_side - field_values)
        - left_coupling * (field_values - left_side)
        + field_values
        - cubic
    )


def body(slice_starts, coupling):
    node_times, matrix = collocation(M)
    weights = jnp.asarray(matrix, jnp.float32)
    diag_weights = jnp.asarray([time_step * moment / M for moment in node_times], jnp.float32)
    node_pos = lax.axis_index("node")
    slice_pos = lax.axis_index("tm")
    systems, cells = coupling.shape
    initial = slice_starts[0]
    implicit = diag_weights[node_pos]
    column = weights[:, node_pos]
    node_state = initial
    partials = []
    for sweep_index in range(SWEEPS):
        if sweep_index == 0:
            end_value = initial
        else:
            end_value = spread(node_state, "node", M - 1)
        arrived = passed_along(end_value, "tm", 1)
        start_value = jnp.where(slice_pos == 0, initial, arrived)
        forcing = operator_term(node_state, coupling)
        row_count = systems * lax.axis_size("node")
        blocks = row_count // systems
        factors = lax.dynamic_slice_in_dim(column, jnp.int32(0) // systems, blocks)
        quadrature = lax.psum_scatter(
            (factors[:, None, None] * forcing[None]).reshape(row_count, cells),
            "node",
            scatter_dimension=0,
            tiled=True,
        )
        base = start_value + time_step * quadrature
        defect = base - node_state
        partial_value = jnp.sum(defect * defect, axis=1)
        partials.append(partial_value)
        target = base - implicit * (node_state - node_state * node_state * node_state)
        iterate = node_state
        for newton_step in range(NEWTON):
            cubic = iterate * iterate * iterate
            derivative = 1.0 - implicit + 3.0 * implicit * iterate * iterate
            iterate = iterate - (iterate - implicit * (iterate - cubic) - target) / derivative
        node_state = iterate
    summed = total_of_pieces(jnp.stack(partials), ("tm", "node"))
    cell_total = lax.axis_size("tm") * M * cells
    residual_log = jnp.log(log_floor + summed / cell_total)
    return (node_state[None, None], residual_log)


def solution(mesh):
    placed = (P("tm", None, None), P())
    return jax.shard_map(
        body,
        mesh=mesh,
        in_specs=placed,
        out_specs=(P("tm", "node", None, None), P()),
        check_vma=False,
    )
```

profile of v0, /device:TPU:1, one launch (start us, length us, event | category | flops | bytes accessed | tf_op | source)
XLA Modules:
  0.0 482.1 jit_solution(10093346001306692199)
XLA Ops:
  7.2 0.0 reduce-scatter.4.cloned.1.call-start
  7.2 0.8 fusion.64
  8.0 0.0 copy-start.1
  8.0 5.0 %fusion.65 = (f32[32,16383]{1,0:T(8,128)}, f32[32,16383]{1,0:T(8,128)}) fusion(f32[32,16384]{1,0:T(8,128)} %bitcast.27), kind=kLoop, calls=%fused_computation.96 | loop fusion | bytes 8388096 | tf_op jit(solution)/shard_map/jit(_roll_static)/slice | solution.py:82
  13.1 0.7 dynamic-slice_bitcast_fusion
  13.7 0.1 mul.223
  13.8 0.1 mul.224
  13.9 0.8 slice.52
  14.7 0.0 copy-done.1
  14.7 4.6 fusion
  19.3 4.1 bitcast_multiply_fusion.2
  23.4 0.0 copy-start.2
  23.4 0.0 reduce-scatter.4.cloned.1.call-update
  23.4 0.0 all-reduce.3.cloned.1.call-start
  23.5 4.9 %collective-permute-start = (f32[32,16384]{1,0:T(8,128)S(1)}, f32[32,16384]{1,0:T(8,128)}, u32[]{:S(2)}, u32[]{:S(2)}) collective-permute-start(f32[32,16384]{1,0:T(8,128)S(1)} %bitcast.28), channel_id=1, source_target_pairs={{0,4},{4,8},{8,12},{12,16},{16,20},{20,24},{24,28},{28,32},{32,36}... | collective-permute-start | bytes 6291464 | tf_op jit(solution)/shard_map/ppermute | solution.py:23
  28.4 0.0 copy-done.2
  28.4 0.6 dynamic_slice.4
  30.3 21.0 %collective-permute-done = f32[32,16384]{1,0:T(8,128)} collective-permute-done((f32[32,16384]{1,0:T(8,128)S(1)}, f32[32,16384]{1,0:T(8,128)}, u32[]{:S(2)}, u32[]{:S(2)}) %collective-permute-start) | collective-permute-done | bytes 2097184 | tf_op jit(solution)/shard_map/ppermute | solution.py:23
  51.4 55.8 %reduce-scatter.4.cloned.1.call-done = f32[32,16384]{1,0:T(8,128)} async-done(((f32[128,16384]{1,0:T(8,128)}), f32[32,16384]{1,0:T(8,128)}) %reduce-scatter.4.cloned.1.call-update) | async-done | bytes 2097168 | tf_op jit(solution)/shard_map/reduce_scatter | solution.py:116
  107.2 5.8 %broadcast_select_fusion.1 = (f32[32,16384]{1,0:T(8,128)}, f32[32,16384]{1,0:T(8,128)S(1)}, f32[32]{0:T(128)S(1)}) fusion(pred[]{:T(512)S(6)} %eq.10, f32[]{:T(128)S(6)} %mul.232, f32[]{:T(128)S(6)} %sub.149, f32[32,16384]{1,0:T(8,128)} %reduce-scatter.4.cloned.1.call-done, f32[32,16384]{1,0:T(8,128)} %collective-permute-done, pred[]{:T(512)S(6)} %eq.4, ...), kind=kLoop, calls=%fused_computation.87 | loop fusion | flops 15728608 | bytes 10485902 | tf_op jit(solution)/shard_map/jit(_where)/select_n | solution.py:17
  113.0 0.0 copy-start
  113.0 0.1 fusion.62
  113.1 2.6 fusion.63
  115.7 0.0 all-reduce.3.cloned.1.call-update
  115.7 0.0 reduce-scatter.6.cloned.1.call-start
  115.8 4.6 fusion.2
  120.4 4.1 bitcast_multiply_fusion.1
  124.5 0.0 reduce-scatter.6.cloned.1.call-update
  124.5 0.0 all-reduce.5.cloned.1.call-start
  124.5 49.6 %all-reduce.3.cloned.1.call-done = f32[32,16384]{1,0:T(8,128)} async-done(((f32[32,16384]{1,0:T(8,128)}), f32[32,16384]{1,0:T(8,128)}) %all-reduce.3.cloned.1.call-update) | async-done | bytes 2097168 | tf_op jit(solution)/shard_map/psum | solution.py:17
  174.1 3.9 collective-permute-start.1
  178.0 23.3 %collective-permute-done.1 = f32[32,16384]{1,0:T(8,128)} collective-permute-done((f32[32,16384]{1,0:T(8,128)}, f32[32,16384]{1,0:T(8,128)}, u32[]{:S(2)}, u32[]{:S(2)}) %collective-permute-start.1) | collective-permute-done | bytes 2097184 | tf_op jit(solution)/shard_map/ppermute | solution.py:23
  201.3 55.7 %reduce-scatter.6.cloned.1.call-done = f32[32,16384]{1,0:T(8,128)} async-done(((f32[128,16384]{1,0:T(8,128)}), f32[32,16384]{1,0:T(8,128)}) %reduce-scatter.6.cloned.1.call-update) | async-done | bytes 2097168 | tf_op jit(solution)/shard_map/reduce_scatter | solution.py:116
  257.0 0.0 copy-done
  257.0 3.4 multiply_reduce_fusion.1
  260.4 4.6 broadcast_select_fusion
  265.0 0.1 fusion.60
  265.1 2.6 fusion.61
  267.7 0.0 all-reduce.5.cloned.1.call-update
  267.8 0.0 reduce-scatter.8.cloned.1.call-start
  267.8 4.6 fusion.4
  272.4 4.1 bitcast_multiply_fusion
  276.5 0.0 reduce-scatter.8.cloned.1.call-update
  276.5 49.6 %all-reduce.5.cloned.1.call-done = f32[32,16384]{1,0:T(8,128)} async-done(((f32[32,16384]{1,0:T(8,128)}), f32[32,16384]{1,0:T(8,128)}) %all-reduce.5.cloned.1.call-update) | async-done | bytes 2097168 | tf_op jit(solution)/shard_map/psum | solution.py:17
  326.1 3.9 collective-permute-start.2
  330.0 23.3 %collective-permute-done.2 = f32[32,16384]{1,0:T(8,128)} collective-permute-done((f32[32,16384]{1,0:T(8,128)}, f32[32,16384]{1,0:T(8,128)}, u32[]{:S(2)}, u32[]{:S(2)}) %collective-permute-start.2) | collective-permute-done | bytes 2097184 | tf_op jit(solution)/shard_map/ppermute | solution.py:23
  353.3 55.6 %reduce-scatter.8.cloned.1.call-done = f32[32,16384]{1,0:T(8,128)} async-done(((f32[128,16384]{1,0:T(8,128)}), f32[32,16384]{1,0:T(8,128)}) %reduce-scatter.8.cloned.1.call-update) | async-done | bytes 2097168 | tf_op jit(solution)/shard_map/reduce_scatter | solution.py:116
  408.9 3.4 multiply_reduce_fusion
  412.3 3.4 fusion.57
  415.7 59.1 %all-gather.1 = f32[128,3,32]{2,1,0:T(4,128)S(1)} all-gather(f32[1,3,32]{2,1,0:T(4,128)S(1)} %maximum_bitcast_fusion), channel_id=2, replica_groups=mesh['tm'=32,'node'=4] {'tm','node'}, dimensions={0}, use_global_device_ids=true | all-gather | bytes 49536 | tf_op jit(solution)/shard_map/all_gather | solution.py:27
  474.8 0.1 reduce_sum.39
  474.9 0.6 add_log_fusion
  (1 shorter events, 0.0 us)
Async XLA Ops:
  7.2 100.0 %reduce-scatter.4.cloned.1.call-start = ((), (), s32[]{:S(2)}) async-start(), calls=%async_computation.3 | async-start | bytes 10485760 | tf_op jit(solution)/shard_map/reduce_scatter | solution.py:116
  8.0 6.7 %copy-start.1 = (f32[1,32,16384]{2,1,0:T(8,128)S(1)}, f32[1,32,16384]{2,1,0:T(8,128)}, u32[]{:S(2)}) copy-start(f32[1,32,16384]{2,1,0:T(8,128)} %param.4) | copy-start | bytes 6291460
  23.4 5.0 %copy-start.2 = (f32[4]{0:T(128)S(1)}, f32[4]{0:T(128)}, u32[]{:S(2)}) copy-start(f32[4]{0:T(128)} %constant.47.clone) | copy-start | bytes 52
  23.4 150.7 %all-reduce.3.cloned.1.call-start = ((), (), s32[]{:S(2)}) async-start(), calls=%async_computation.4 | async-start | bytes 4194304 | tf_op jit(solution)/shard_map/psum | solution.py:17
  23.5 27.9 %collective-permute-start = (f32[32,16384]{1,0:T(8,128)S(1)}, f32[32,16384]{1,0:T(8,128)}, u32[]{:S(2)}, u32[]{:S(2)}) collective-permute-start(f32[32,16384]{1,0:T(8,128)S(1)} %bitcast.28), channel_id=1, source_target_pairs={{0,4},{4,8},{8,12},{12,16},{16,20},{20,24},{24,28},{28,32},{32,36}... | collective-permute-start | bytes 6291464 | tf_op jit(solution)/shard_map/ppermute | solution.py:23
  113.0 144.0 %copy-start = (f32[32,16384]{1,0:T(8,128)}, f32[32,16384]{1,0:T(8,128)S(1)}, u32[]{:S(2)}) copy-start(f32[32,16384]{1,0:T(8,128)S(1)} %get-tuple-element.9) | copy-start | bytes 6291460
  115.7 141.3 %reduce-scatter.6.cloned.1.call-start = ((), (), s32[]{:S(2)}) async-start(), calls=%async_computation.5 | async-start | bytes 10485760 | tf_op jit(solution)/shard_map/reduce_scatter | solution.py:116
  124.5 201.7 %all-reduce.5.cloned.1.call-start = ((), (), s32[]{:S(2)}) async-start(), calls=%async_computation.6 | async-start | bytes 4194304 | tf_op jit(solution)/shard_map/psum | solution.py:17
  174.1 27.2 %collective-permute-start.1 = (f32[32,16384]{1,0:T(8,128)}, f32[32,16384]{1,0:T(8,128)}, u32[]{:S(2)}, u32[]{:S(2)}) collective-permute-start(f32[32,16384]{1,0:T(8,128)} %all-reduce.3.cloned.1.call-done), channel_id=1, source_target_pairs={{0,4},{4,8},{8,12},{12,16},{16,20},{20,24},{24,28},{28,32},{32,36}... | collective-permute-start | bytes 6291464 | tf_op jit(solution)/shard_map/ppermute | solution.py:23
  267.8 141.2 %reduce-scatter.8.cloned.1.call-start = ((), (), s32[]{:S(2)}) async-start(), calls=%async_computation.7 | async-start | bytes 10485760 | tf_op jit(solution)/shard_map/reduce_scatter | solution.py:116
  326.1 27.2 %collective-permute-start.2 = (f32[32,16384]{1,0:T(8,128)}, f32[32,16384]{1,0:T(8,128)}, u32[]{:S(2)}, u32[]{:S(2)}) collective-permute-start(f32[32,16384]{1,0:T(8,128)} %all-reduce.5.cloned.1.call-done), channel_id=1, source_target_pairs={{0,4},{4,8},{8,12},{12,16},{16,20},{20,24},{24,28},{28,32},{32,36}... | collective-permute-start | bytes 6291464 | tf_op jit(solution)/shard_map/ppermute | solution.py:23
Sparse Core Ops, SparseCore 0:
  23.5 83.6 reduce-scatter.3
  115.8 58.2 all-reduce.2
  176.6 80.3 reduce-scatter.5
  267.9 58.2 all-reduce.4
  328.5 80.3 reduce-scatter.7
where the time goes:
time: 484 us; the launch traced here: 482 us
  waiting for transfers between devices  334 us (69%)
  blocking collectives  59.1 us (12%)
  other arithmetic  47.4 us (10%)
  between operations  15.2 us (3%)
  local copies, waits for them, and re-layouts  13.4 us (3%)
  starting transfers between devices  12.9 us (3%)
    reduce_scatter x3, waiting for transfers between devices, body(): lax.psum_scatter((factors[:, None, None] * forcing[None]).reshape(row_cou...  167 us
    psum x2, waiting for transfers between devices, spread(): return lax.psum(jnp.where(mine, value, jnp.zeros_like(value)), axis)  99.2 us
    ppermute x3, waiting for transfers between devices, passed_along(): return lax.ppermute(value, axis, pairs)  67.6 us
    all_gather x1, blocking collectives, total_of_pieces(): return lax.all_gather(value, axis).sum(0)  59.1 us
    sub x3, other arithmetic, operator_term(): coupling * (right_side - field_values)  13.9 us
    ppermute x3, starting transfers between devices, passed_along(): return lax.ppermute(value, axis, pairs)  12.7 us
    mul x3, other arithmetic, body(): factors[:, None, None] * forcing[None]  12.2 us
    slice x6, local copies, waits for them, and re-layouts, operator_term(): left_side = jnp.roll(field_values, 1, axis=-1)  11.2 us
  transfers between devices with their start and end apart: 8, of which 8 were waited for; matrix products, arithmetic and copies ran while one was open for 4% of the time, Pallas kernels for 0%

commit v1 on v0

v1 whole, which is shorter than its diff:
```python
import functools

import jax
import jax.numpy as jnp
import numpy as np
from jax import lax
from jax.experimental import pallas as pl
from jax.experimental.pallas import tpu as pltpu
from jax.sharding import PartitionSpec as P

M = 4
SWEEPS = 3
CORES = 2
LANES = 128
ROWS = 8
TILE = 4
PAD = 5
time_step = 0.5
log_floor = 0.05


def legendre_gap(point, node_count):
    before = 1.0
    current = point
    for degree in range(1, node_count):
        following = ((2 * degree + 1) * point * current - degree * before) / (degree + 1)
        before = current
        current = following
    return current - before


def collocation(node_count):
    points = []
    samples = 4000
    for sample_index in range(samples - 1):
        lower_end = -1.0 + 2.0 * sample_index / samples
        upper_end = -1.0 + 2.0 * (sample_index + 1) / samples
        lower_value = legendre_gap(lower_end, node_count)
        upper_value = legendre_gap(upper_end, node_count)
        if lower_value * upper_value < 0.0:
            for halving in range(80):
                middle = 0.5 * (lower_end + upper_end)
                middle_value = legendre_gap(middle, node_count)
                if lower_value * middle_value <= 0.0:
                    upper_end = middle
                else:
                    lower_end = middle
                    lower_value = middle_value
            points.append(0.5 * (lower_end + upper_end))
    points.append(1.0)
    node_times = [(point + 1.0) / 2.0 for point in points]
    matrix = [[0.0] * node_count for row_index in range(node_count)]
    for column in range(node_count):
        coeffs = [1.0]
        for other in range(node_count):
            if other != column:
                scale = node_times[column] - node_times[other]
                shifted = [0.0] + coeffs
                scaled = [value * node_times[other] for value in coeffs] + [0.0]
                coeffs = [(shifted[power] - scaled[power]) / scale for power in range(len(shifted))]
        for row_index in range(node_count):
            upper_time = node_times[row_index]
            matrix[row_index][column] = sum(
                coeffs[power] * upper_time ** (power + 1) / (power + 1) for power in range(len(coeffs))
            )
    return (node_times, matrix)


NODE_TIMES, MATRIX = collocation(M)
WEIGHTS = [[time_step * float(np.float32(q)) for q in row] for row in MATRIX]
IMPLICIT = [float(np.float32(time_step * t / M)) for t in NODE_TIMES]
ROW_SUMS = [sum(row) for row in WEIGHTS]


def kernel(sizes, ss_ref, cp_ref, out_ref, res_ref, buf, cbuf, u1, e1, u2, e2, rbuf, acc, st1, st2, st3,
           csem, rsem, zsend, osend, orecv, s1s, s1r, s2s, s2r, s3s, s3r):
    ny, nz, cells, mean_count = sizes
    half = cells // LANES // CORES
    tiles = half // TILE
    whole = cells // LANES
    chips = ny * nz
    tm = lax.axis_index("tm")
    node = lax.axis_index("node")
    core = lax.rem(tm, CORES)
    chip = lax.div(tm, CORES)
    zpos = lax.rem(chip, nz)
    ypos = lax.div(chip, nz)
    rows = pl.ds(pl.multiple_of(node * ROWS, ROWS), ROWS)

    def at_chip(by, which):
        return lax.rem(chip + by + 2 * chips, chips) * CORES + which

    def at_zcore(slot):
        return ypos * (nz * CORES) + slot

    def at_y(slot):
        return slot * (nz * CORES) + lax.rem(tm, nz * CORES)

    def cols(start, count):
        if isinstance(start, int):
            return pl.ds(start * LANES, count * LANES)
        return pl.ds(pl.multiple_of(start * LANES, LANES), count * LANES)

    def remote(src, dst, send, recv, to_tm, to_node):
        return pltpu.make_async_remote_copy(
            src, dst, send, recv, device_id=(to_tm, to_node), device_id_type=pl.DeviceIdType.MESH
        )

    def source(which, a):
        if isinstance(a, int) and a == 0:
            return lax.rem(half * which + whole - 1, whole), PAD - 1, 1
        return lax.rem(half * which + TILE * (a - 1), whole), PAD + TILE * (a - 1), TILE

    def local_set(a):
        start, q, count = source(core, a)
        pltpu.make_async_copy(cp_ref.at[rows, cols(start, count)], cbuf.at[:, cols(q, count)], csem.at[a]).start()
        pltpu.make_async_copy(
            ss_ref.at[0, rows, cols(start, count)], buf.at[3 + core, :, cols(q, count)], rsem.at[3 + core, a]
        ).start()

    def remote_set(a):
        @pl.when(core == 1)
        def _():
            for which in range(CORES):
                start, q, count = source(which, a)
                remote(ss_ref.at[0, rows, cols(start, count)], buf.at[0, :, cols(q, count)],
                       zsend.at[2 + which], rsem.at[0, a], at_chip(2, which), node).start()

        for which in range(CORES):
            start, q, count = source(which, a)
            remote(ss_ref.at[0, rows, cols(start, count)], buf.at[1 + core, :, cols(q, count)],
                   zsend.at[which], rsem.at[1 + core, a], at_chip(1, which), node).start()
        start, q, count = source(1 - core, a)
        remote(ss_ref.at[0, rows, cols(start, count)], buf.at[3 + core, :, cols(q, count)],
               zsend.at[4], rsem.at[3 + core, a], at_chip(0, 1 - core), node).start()

    def wait_set(a):
        _, q, count = source(core, a)
        pltpu.make_async_copy(cbuf.at[:, cols(q, count)], cbuf.at[:, cols(q, count)], csem.at[a]).wait()
        for n in range(5):
            view = buf.at[n, :, cols(q, count)]
            pltpu.make_async_copy(view, view, rsem.at[n, a]).wait()

    local_set(0)

    @pl.loop(1, tiles + 2)
    def _(a):
        local_set(a)

    barrier = pltpu.get_barrier_semaphore()
    greeted = 0

    def greet(to_tm, to_node):
        pl.semaphore_signal(barrier, inc=1, device_id=(to_tm, to_node), device_id_type=pl.DeviceIdType.MESH)

    greet(at_chip(0, 1 - core), node)
    greeted += 1
    for by in range(1, M):
        for which in range(CORES):
            greet(at_chip(0, which), lax.rem(node + by, M))
            greeted += 1
    for by in (1, 2, -1, -2):
        for which in range(CORES):
            greet(at_chip(by, which), node)
            greeted += 1
    for by in range(1, nz):
        for which in range(CORES):
            greet(at_zcore(lax.rem(zpos + by, nz) * CORES + which), node)
            greeted += 1
    for by in range(1, ny):
        greet(at_y(lax.rem(ypos + by, ny)), node)
        greeted += 1
    pl.semaphore_wait(barrier, greeted)

    remote_set(0)

    @pl.loop(1, tiles + 2)
    def _(a):
        remote_set(a)

    acc[...] = jnp.zeros_like(acc)
    first = chip == 0
    second = chip == 1
    width = TILE * LANES

    def force(ref, q, cw):
        x = ref[:, cols(q - 1, TILE + 2)]
        flux = cw * (pltpu.roll(x, (TILE + 2) * LANES - 1, axis=1) - x)
        spread = flux - pltpu.roll(flux, 1, axis=1)
        u = x[:, LANES:LANES + width]
        square = u * u
        g = u - u * square
        return u, square, g, spread[:, LANES:LANES + width] + g

    def newton(u, square, g, base, m):
        a = IMPLICIT[m]
        defect = base - u
        target = base - a * g
        once = u + defect / ((1.0 - a) + (3.0 * a) * square)
        square = once * once
        twice = (target + (2.0 * a) * square * once) / ((1.0 - a) + (3.0 * a) * square)
        return twice, defect

    def add_up(k, q, total):
        parts = []
        for t in range(TILE):
            mine = jnp.logical_and(q + t >= PAD, q + t < PAD + half)
            part = total[:, t * LANES:(t + 1) * LANES]
            parts.append(jnp.where(mine, part, jnp.zeros_like(part)))
        acc[k] += (parts[0] + parts[1]) + (parts[2] + parts[3])

    def start_sweep(q):
        cw = cbuf[:, cols(q - 1, TILE + 2)]
        here = cols(q, TILE)
        total = None
        for n in range(1, 5):
            u, square, g, f = force(buf.at[n], q, cw)
            before = buf[n - 1, :, here]
            if n == 3:
                before = jnp.where(first, u, before)
            if n == 1:
                before = jnp.where(second, u, before)
            for m in range(M):
                if n == 1 and m < M - 1:
                    continue
                new, defect = newton(u, square, g, before + ROW_SUMS[m] * f, m)
                if n == 1:
                    e1[:, here] = new
                else:
                    u1[n - 2, m, :, here] = new
                if n >= 3:
                    total = defect * defect if total is None else total + defect * defect
        add_up(0, q, total)

    def later_sweep(k, q):
        cw = cbuf[:, cols(q - 1, TILE + 2)]
        here = cols(q, TILE)
        total = None
        old = u1 if k == 1 else u2
        for n in range(2 if k == 1 else 3, 5):
            slot = n - 2 if k == 1 else n - 3
            parts = [force(old.at[slot, m], q, cw) for m in range(M)]
            if n == 2:
                before = e1[:, here]
            elif n == 3:
                before = u1[0, M - 1, :, here] if k == 1 else e2[:, here]
                before = jnp.where(first, buf[3, :, here], before)
            else:
                before = old[slot - 1, M - 1, :, here]
            for m in range(M):
                if n == 2 and m < M - 1:
                    continue
                base = before
                for j in range(M):
                    base = base + WEIGHTS[m][j] * parts[j][3]
                new, defect = newton(parts[m][0], parts[m][1], parts[m][2], base, m)
                if n == 2:
                    e2[:, here] = new
                elif k == 1:
                    u2[n - 3, m, :, here] = new
                else:
                    rbuf[n - 3, m, :, here] = new
                if n >= 3:
                    total = defect * defect if total is None else total + defect * defect
        add_up(k, q, total)

    def send_out(i):
        q = PAD + TILE * i
        place = cols(core * half + TILE * i, TILE)
        for away in range(M):
            to_node = lax.rem(node + away, M)
            for other in range(CORES):
                which = core if other == 0 else 1 - core
                src = rbuf.at[which, to_node, :, cols(q, TILE)]
                dst = out_ref.at[0, 0, rows, place]
                if away == 0 and other == 0:
                    pltpu.make_async_copy(src, dst, osend.at[0, 0]).start()
                else:
                    remote(src, dst, osend.at[other, away], orecv.at[other, away],
                           at_chip(0, which), to_node).start()

    wait_set(0)

    @pl.loop(0, tiles + 1)
    def _(step):
        i = step - 1
        wait_set(step + 1)
        q = PAD + TILE * i
        start_sweep(q + 2)
        later_sweep(1, q + 1)
        later_sweep(2, q)

        @pl.when(step > 0)
        def _():
            send_out(i)

    lane = lax.broadcasted_iota(jnp.int32, (ROWS, LANES), 1)
    sums = jnp.zeros((ROWS, LANES), jnp.float32)
    for k in range(SWEEPS):
        sums = jnp.where(lane == k, jnp.sum(acc[k], axis=1, keepdims=True), sums)
    zcore = lax.rem(tm, nz * CORES)
    st1[zcore] = sums
    flows = []
    for by in range(1, nz * CORES):
        to = at_zcore(lax.rem(zcore + by, nz * CORES))
        c = remote(st1.at[zcore], st1.at[zcore], s1s.at[by], s1r.at[by], to, node)
        c.start()
        flows.append(c)
    for c in flows:
        c.wait()
    sums = st1[0]
    for slot in range(1, nz * CORES):
        sums = sums + st1[slot]
    st2[ypos] = sums
    flows = []
    for by in range(1, ny):
        c = remote(st2.at[ypos], st2.at[ypos], s2s.at[by], s2r.at[by], at_y(lax.rem(ypos + by, ny)), node)
        c.start()
        flows.append(c)
    for c in flows:
        c.wait()
    sums = st2[0]
    for slot in range(1, ny):
        sums = sums + st2[slot]
    st3[node] = sums
    flows = []
    for by in range(1, M):
        c = remote(st3.at[node], st3.at[node], s3s.at[by], s3r.at[by], tm, lax.rem(node + by, M))
        c.start()
        flows.append(c)
    for c in flows:
        c.wait()
    table = jnp.concatenate([st3[m] for m in range(M)] + [jnp.zeros((LANES - M * ROWS, LANES), jnp.float32)], axis=0)
    table = jnp.log(log_floor + table.T / mean_count)
    res_ref[...] = table[:SWEEPS, :M * ROWS]

    sent = buf.at[0, :, cols(0, 1 + TILE * (tiles + 1))]
    for flow in (0, 1, 4):
        pltpu.make_async_copy(sent, sent, zsend.at[flow]).wait()

    @pl.when(core == 1)
    def _():
        for flow in (2, 3):
            pltpu.make_async_copy(sent, sent, zsend.at[flow]).wait()

    made = rbuf.at[0, 0, :, cols(0, half)]
    for away in range(M):
        for other in range(CORES):
            pltpu.make_async_copy(made, made, osend.at[other, away]).wait()
            if away or other:
                pltpu.make_async_copy(made, made, orecv.at[other, away]).wait()


def body(sizes, slice_starts, coupling):
    systems, cells = coupling.shape
    ny, nz = sizes
    half = cells // LANES // CORES
    tiles = half // TILE
    span = half + PAD + TILE
    mean_count = float(ny * nz * CORES * M * cells)
    flat = lambda *lead: pltpu.VMEM(lead + (ROWS, span * LANES), jnp.float32)
    dma = pltpu.SemaphoreType.DMA
    any_spec = pl.BlockSpec(memory_space=pl.ANY)
    return pl.pallas_call(
        functools.partial(kernel, (ny, nz, cells, mean_count)),
        out_shape=(
            jax.ShapeDtypeStruct((1, 1, systems, cells), jnp.float32),
            jax.ShapeDtypeStruct((SWEEPS, systems), jnp.float32),
        ),
        in_specs=[any_spec, any_spec],
        out_specs=(any_spec, pl.BlockSpec(memory_space=pltpu.VMEM)),
        scratch_shapes=[
            flat(5), flat(), flat(3, M), flat(), flat(2, M), flat(), flat(2, M),
            pltpu.VMEM((SWEEPS, ROWS, LANES), jnp.float32),
            pltpu.VMEM((nz * CORES, ROWS, LANES), jnp.float32),
            pltpu.VMEM((ny, ROWS, LANES), jnp.float32),
            pltpu.VMEM((M, ROWS, LANES), jnp.float32),
            dma((tiles + 2,)), dma((5, tiles + 2)), dma((5,)), dma((CORES, M)), dma((CORES, M)),
            dma((nz * CORES,)), dma((nz * CORES,)), dma((ny,)), dma((ny,)), dma((M,)), dma((M,)),
        ],
        compiler_params=pltpu.CompilerParams(
            collective_id=0, has_side_effects=True, vmem_limit_bytes=48 * 2**20
        ),
        name="sdc",
    )(slice_starts, coupling)


def solution(mesh):
    chips = mesh.shape["tm"] // CORES
    ny = 4
    return jax.shard_map(
        functools.partial(body, (ny, chips // ny)),
        mesh=mesh,
        in_specs=(P("tm", None, None), P()),
        out_specs=(P("tm", "node", None, None), P()),
        check_vma=False,
    )
```

time: 484 us -> 49.8 us (0.10)
  waiting for transfers between devices: 334 us -> 0 us
  blocking collectives: 59.1 us -> 0 us
  other arithmetic: 47.4 us -> 0 us
  Pallas kernels: 0 us -> 45.6 us
  between operations: 15.2 us -> 0.65 us
  starting transfers between devices: 12.9 us -> 0 us
  local copies, waits for them, and re-layouts: 13.4 us -> 3.48 us
    reduce_scatter x3 -> x0, waiting for transfers between devices: 167 us -> none  [body(): lax.psum_scatter((factors[:, None, None] * forcing[None]).reshape(row_cou...]
    psum x2 -> x0, waiting for transfers between devices: 99.2 us -> none  [spread(): return lax.psum(jnp.where(mine, value, jnp.zeros_like(value)), axis)]
    ppermute x3 -> x0, waiting for transfers between devices: 67.6 us -> none  [passed_along(): return lax.ppermute(value, axis, pairs)]
    all_gather x1 -> x0, blocking collectives: 59.1 us -> none  [total_of_pieces(): return lax.all_gather(value, axis).sum(0)]
    pallas_call x0 -> x1, Pallas kernels: none -> 45.6 us  [body(): pl.pallas_call(functools.partial(kernel, (ny, nz, cells, mean_count)), ou...]
    sub x3 -> x0, other arithmetic: 13.9 us -> none  [operator_term(): coupling * (right_side - field_values)]
    ppermute x3 -> x0, starting transfers between devices: 12.7 us -> none  [passed_along(): return lax.ppermute(value, axis, pairs)]
    mul x3 -> x0, other arithmetic: 12.2 us -> none  [body(): factors[:, None, None] * forcing[None]]
  transfers between devices with their start and end apart: 8 -> 0, of which waited for: 8 -> 0; matrix products, arithmetic and copies ran while one was open for 4% -> 0% of each run, Pallas kernels for 0% -> 0%
where the time goes in v1:
time: 49.8 us; the launch traced here: 49.7 us
  Pallas kernels  45.6 us (92%)
  local copies, waits for them, and re-layouts  3.48 us (7%)
  between operations  0.65 us (1%)
    pallas_call x1, Pallas kernels, body(): pl.pallas_call(functools.partial(kernel, (ny, nz, cells, mean_count)), ou...  45.6 us
    unnamed x4, local copies, waits for them, and re-layouts  3.48 us

profile of v1, /device:TPU:1, one launch (start us, length us, event | category | flops | bytes accessed | tf_op | source)
XLA Modules:
  0.0 49.7 jit_solution(6841435253172325981)
XLA Ops:
  0.6 0.0 copy-start
  0.6 1.6 %copy-done = f32[1,32,16384]{2,1,0:T(8,128)S(1)} copy-done((f32[1,32,16384]{2,1,0:T(8,128)S(1)}, f32[1,32,16384]{2,1,0:T(8,128)}, u32[]{:S(2)}) %copy-start) | copy-done | bytes 2097176
  2.2 45.6 %sdc.1 = (f32[1,1,32,16384]{3,2,1,0:T(8,128)S(1)}, f32[3,32]{1,0:T(4,128)S(1)}) custom-call(f32[1,32,16384]{2,1,0:T(8,128)S(1)} %copy-done, f32[32,16384]{1,0:T(8,128)} %cp_ref.1), custom_call_target="tpu_custom_call" | custom-call | tf_op jit(solution)/shard_map/sdc/pallas_call | solution.py:364
  47.8 1.3 %copy.6 = f32[1,1,32,16384]{3,2,1,0:T(8,128)} copy(f32[1,1,32,16384]{3,2,1,0:T(8,128)S(1)} %get-tuple-element.4) | data formatting | bytes 4194304
  49.1 0.6 %copy.7 = f32[3,32]{1,0:T(4,128)} copy(f32[3,32]{1,0:T(4,128)S(1)} %get-tuple-element.5) | data formatting | bytes 768
Async XLA Ops:
  0.6 1.6 %copy-start = (f32[1,32,16384]{2,1,0:T(8,128)S(1)}, f32[1,32,16384]{2,1,0:T(8,128)}, u32[]{:S(2)}) copy-start(f32[1,32,16384]{2,1,0:T(8,128)} %ss_ref.1) | copy-start | bytes 6291460

commit v2 on v1

--- a/solution.py
+++ b/solution.py
@@ -72,13 +72,18 @@
 ROW_SUMS = [sum(row) for row in WEIGHTS]
 
 
-def kernel(sizes, ss_ref, cp_ref, out_ref, res_ref, buf, cbuf, u1, e1, u2, e2, rbuf, acc, st1, st2, st3,
-           csem, rsem, zsend, osend, orecv, s1s, s1r, s2s, s2r, s3s, s3r):
+DIRECT = 5
+LEAD = 5
+
+
+def kernel(sizes, ss_ref, cp_ref, out_ref, res_ref, own, transit, buf, cbuf, u1, e1, u2, e2, rbuf, acc, st1, st2, st3,
+           wsem, csem, rsem, tsem, zsend, osend, orecv, s1s, s1r, s2s, s2r, s3s, s3r):
     ny, nz, cells, mean_count = sizes
     half = cells // LANES // CORES
     tiles = half // TILE
     whole = cells // LANES
     chips = ny * nz
+    sets = tiles + 2
     tm = lax.axis_index("tm")
     node = lax.axis_index("node")
     core = lax.rem(tm, CORES)
@@ -87,14 +92,19 @@
     ypos = lax.div(chip, nz)
     rows = pl.ds(pl.multiple_of(node * ROWS, ROWS), ROWS)
 
-    def at_chip(by, which):
-        return lax.rem(chip + by + 2 * chips, chips) * CORES + which
-
-    def at_zcore(slot):
-        return ypos * (nz * CORES) + slot
-
-    def at_y(slot):
-        return slot * (nz * CORES) + lax.rem(tm, nz * CORES)
+    middle = jnp.where(zpos == 0, chip + nz - 1, chip - 1)
+    source_chip = jnp.where(zpos == nz - 1, chip - nz + 1, chip + 1)
+    target = jnp.where(zpos == nz - 1, chip - 1, chip + nz - 1)
+    middle_of_target = jnp.where(zpos == 2, chip + 1, chip - nz + 1)
+    has_next = chip < chips - 1
+    has_before = chip > 0
+    far_source = jnp.logical_and(core == 1, chip < chips - 2)
+    far_target = chip > 1
+    is_middle = source_chip < chips - 2
+    far_middle = jnp.logical_and(core == 0, is_middle)
+
+    def dev(which_chip, which):
+        return which_chip * CORES + which
 
     def cols(start, count):
         if isinstance(start, int):
@@ -118,65 +128,116 @@
             ss_ref.at[0, rows, cols(start, count)], buf.at[3 + core, :, cols(q, count)], rsem.at[3 + core, a]
         ).start()
 
-    def remote_set(a):
-        @pl.when(core == 1)
+    def near_set(a):
+        @pl.when(has_next)
         def _():
             for which in range(CORES):
                 start, q, count = source(which, a)
-                remote(ss_ref.at[0, rows, cols(start, count)], buf.at[0, :, cols(q, count)],
-                       zsend.at[2 + which], rsem.at[0, a], at_chip(2, which), node).start()
-
+                remote(own.at[:, cols(start, count)], buf.at[1 + core, :, cols(q, count)],
+                       zsend.at[which], rsem.at[1 + core, a], dev(chip + 1, which), node).start()
+
+        start, q, count = source(1 - core, a)
+        remote(own.at[:, cols(start, count)], buf.at[3 + core, :, cols(q, count)],
+               zsend.at[4], rsem.at[3 + core, a], dev(chip, 1 - core), node).start()
+
+    def direct_set(a):
+        @pl.when(far_source)
+        def _():
+            for which in range(CORES):
+                start, q, count = source(which, a)
+                remote(own.at[:, cols(start, count)], buf.at[0, :, cols(q, count)],
+                       zsend.at[2 + which], rsem.at[0, a], dev(chip + 2, which), node).start()
+
+    def first_leg(a):
+        @pl.when(far_source)
+        def _():
+            for which in range(CORES):
+                start, q, count = source(which, a)
+                remote(own.at[:, cols(start, count)], transit.at[which, :, cols(q, count)],
+                       zsend.at[5 + which], tsem.at[which, a], dev(middle, 0), node).start()
+
+    def second_leg(a):
         for which in range(CORES):
-            start, q, count = source(which, a)
-            remote(ss_ref.at[0, rows, cols(start, count)], buf.at[1 + core, :, cols(q, count)],
-                   zsend.at[which], rsem.at[1 + core, a], at_chip(1, which), node).start()
-        start, q, count = source(1 - core, a)
-        remote(ss_ref.at[0, rows, cols(start, count)], buf.at[3 + core, :, cols(q, count)],
-               zsend.at[4], rsem.at[3 + core, a], at_chip(0, 1 - core), node).start()
+            _, q, count = source(which, a)
+            view = transit.at[which, :, cols(q, count)]
+            pltpu.make_async_copy(view, view, tsem.at[which, a]).wait()
+            remote(view, buf.at[0, :, cols(q, count)],
+                   zsend.at[7 + which], rsem.at[0, a], dev(target, which), node).start()
 
     def wait_set(a):
         _, q, count = source(core, a)
         pltpu.make_async_copy(cbuf.at[:, cols(q, count)], cbuf.at[:, cols(q, count)], csem.at[a]).wait()
-        for n in range(5):
+
+        def arrived(n):
             view = buf.at[n, :, cols(q, count)]
             pltpu.make_async_copy(view, view, rsem.at[n, a]).wait()
 
+        arrived(3)
+        arrived(4)
+
+        @pl.when(has_before)
+        def _():
+            arrived(1)
+            arrived(2)
+
+        @pl.when(far_target)
+        def _():
+            arrived(0)
+
+    fetch = pltpu.make_async_copy(ss_ref.at[0, rows, :], own, wsem.at[0])
+    fetch.start()
     local_set(0)
 
-    @pl.loop(1, tiles + 2)
+    @pl.loop(1, sets)
     def _(a):
         local_set(a)
 
     barrier = pltpu.get_barrier_semaphore()
-    greeted = 0
 
     def greet(to_tm, to_node):
         pl.semaphore_signal(barrier, inc=1, device_id=(to_tm, to_node), device_id_type=pl.DeviceIdType.MESH)
 
-    greet(at_chip(0, 1 - core), node)
-    greeted += 1
+    def both(which_chip):
+        for which in range(CORES):
+            greet(dev(which_chip, which), node)
+
+    greeted = jnp.int32(0)
+    for cond, count, hello in (
+        (has_next, 2, lambda: both(chip + 1)),
+        (has_before, 2, lambda: both(chip - 1)),
+        (far_source, 2, lambda: both(chip + 2)),
+        (far_target, 1, lambda: greet(dev(chip - 2, 1), node)),
+        (far_source, 1, lambda: greet(dev(middle, 0), node)),
+        (far_middle, 1, lambda: greet(dev(source_chip, 1), node)),
+        (far_middle, 2, lambda: both(target)),
+        (far_target, 1, lambda: greet(dev(middle_of_target, 0), node)),
+    ):
+        pl.when(cond)(hello)
+        greeted = greeted + jnp.where(cond, count, 0)
+    greet(dev(chip, 1 - core), node)
     for by in range(1, M):
         for which in range(CORES):
-            greet(at_chip(0, which), lax.rem(node + by, M))
-            greeted += 1
-    for by in (1, 2, -1, -2):
-        for which in range(CORES):
-            greet(at_chip(by, which), node)
-            greeted += 1
+            greet(dev(chip, which), lax.rem(node + by, M))
     for by in range(1, nz):
-        for which in range(CORES):
-            greet(at_zcore(lax.rem(zpos + by, nz) * CORES + which), node)
-            greeted += 1
+        greet(dev(ypos * nz + lax.rem(zpos + by, nz), core), node)
     for by in range(1, ny):
-        greet(at_y(lax.rem(ypos + by, ny)), node)
-        greeted += 1
-    pl.semaphore_wait(barrier, greeted)
-
-    remote_set(0)
-
-    @pl.loop(1, tiles + 2)
+        greet(dev(lax.rem(ypos + by, ny) * nz + zpos, core), node)
+    always = CORES * M - 1 + nz - 1 + ny - 1
+    pl.semaphore_wait(barrier, greeted + always)
+    fetch.wait()
+
+    direct_set(0)
+    near_set(0)
+
+    @pl.loop(1, DIRECT + 1)
     def _(a):
-        remote_set(a)
+        direct_set(a)
+        near_set(a)
+
+    @pl.loop(DIRECT + 1, sets)
+    def _(a):
+        first_leg(a)
+        near_set(a)
 
     acc[...] = jnp.zeros_like(acc)
     first = chip == 0
@@ -277,13 +338,18 @@
                     pltpu.make_async_copy(src, dst, osend.at[0, 0]).start()
                 else:
                     remote(src, dst, osend.at[other, away], orecv.at[other, away],
-                           at_chip(0, which), to_node).start()
+                           dev(chip, which), to_node).start()
 
     wait_set(0)
 
     @pl.loop(0, tiles + 1)
     def _(step):
         i = step - 1
+
+        @pl.when(jnp.logical_and(far_middle, step + LEAD + 1 < sets))
+        def _():
+            second_leg(step + LEAD + 1)
+
         wait_set(step + 1)
         q = PAD + TILE * i
         start_sweep(q + 2)
@@ -298,50 +364,54 @@
     sums = jnp.zeros((ROWS, LANES), jnp.float32)
     for k in range(SWEEPS):
         sums = jnp.where(lane == k, jnp.sum(acc[k], axis=1, keepdims=True), sums)
-    zcore = lax.rem(tm, nz * CORES)
-    st1[zcore] = sums
-    flows = []
-    for by in range(1, nz * CORES):
-        to = at_zcore(lax.rem(zcore + by, nz * CORES))
-        c = remote(st1.at[zcore], st1.at[zcore], s1s.at[by], s1r.at[by], to, node)
-        c.start()
-        flows.append(c)
-    for c in flows:
-        c.wait()
-    sums = st1[0]
-    for slot in range(1, nz * CORES):
-        sums = sums + st1[slot]
-    st2[ypos] = sums
-    flows = []
-    for by in range(1, ny):
-        c = remote(st2.at[ypos], st2.at[ypos], s2s.at[by], s2r.at[by], at_y(lax.rem(ypos + by, ny)), node)
-        c.start()
-        flows.append(c)
-    for c in flows:
-        c.wait()
-    sums = st2[0]
-    for slot in range(1, ny):
-        sums = sums + st2[slot]
-    st3[node] = sums
-    flows = []
-    for by in range(1, M):
-        c = remote(st3.at[node], st3.at[node], s3s.at[by], s3r.at[by], tm, lax.rem(node + by, M))
-        c.start()
-        flows.append(c)
-    for c in flows:
-        c.wait()
-    table = jnp.concatenate([st3[m] for m in range(M)] + [jnp.zeros((LANES - M * ROWS, LANES), jnp.float32)], axis=0)
+
+    def swap(store, mine, value, peers, send, recv):
+        store[mine] = value
+        flows = [
+            remote(store.at[mine], store.at[mine], send.at[by], recv.at[by], to_tm, to_node)
+            for by, (to_tm, to_node) in enumerate(peers)
+        ]
+        for c in flows:
+            c.start()
+        for c in flows:
+            c.wait()
+
+    swap(st1, zpos, sums, [(dev(ypos * nz + lax.rem(zpos + by, nz), core), node) for by in range(1, nz)], s1s, s1r)
+    sums = (st1[0] + st1[1]) + (st1[2] + st1[3])
+    swap(st2, ypos, sums, [(dev(lax.rem(ypos + by, ny) * nz + zpos, core), node) for by in range(1, ny)], s2s, s2r)
+    sums = (st2[0] + st2[1]) + (st2[2] + st2[3])
+    me = node * CORES + core
+    peers = [lax.rem(me + by, M * CORES) for by in range(1, M * CORES)]
+    swap(st3, me, sums, [(dev(chip, lax.rem(p, CORES)), lax.div(p, CORES)) for p in peers], s3s, s3r)
+    table = jnp.concatenate(
+        [st3[CORES * m] + st3[CORES * m + 1] for m in range(M)]
+        + [jnp.zeros((LANES - M * ROWS, LANES), jnp.float32)],
+        axis=0,
+    )
     table = jnp.log(log_floor + table.T / mean_count)
     res_ref[...] = table[:SWEEPS, :M * ROWS]
 
-    sent = buf.at[0, :, cols(0, 1 + TILE * (tiles + 1))]
-    for flow in (0, 1, 4):
-        pltpu.make_async_copy(sent, sent, zsend.at[flow]).wait()
-
-    @pl.when(core == 1)
+    def ended(flow, count):
+        view = own.at[:, cols(0, count)]
+        pltpu.make_async_copy(view, view, zsend.at[flow]).wait()
+
+    ended(4, 1 + TILE * (sets - 1))
+
+    @pl.when(has_next)
     def _():
-        for flow in (2, 3):
-            pltpu.make_async_copy(sent, sent, zsend.at[flow]).wait()
+        ended(0, 1 + TILE * (sets - 1))
+        ended(1, 1 + TILE * (sets - 1))
+
+    @pl.when(far_source)
+    def _():
+        for which in range(CORES):
+            ended(2 + which, 1 + TILE * DIRECT)
+            ended(5 + which, TILE * (sets - 1 - DIRECT))
+
+    @pl.when(far_middle)
+    def _():
+        for which in range(CORES):
+            ended(7 + which, TILE * (sets - 1 - DIRECT))
 
     made = rbuf.at[0, 0, :, cols(0, half)]
     for away in range(M):
@@ -367,16 +437,18 @@
             jax.ShapeDtypeStruct((1, 1, systems, cells), jnp.float32),
             jax.ShapeDtypeStruct((SWEEPS, systems), jnp.float32),
         ),
-        in_specs=[any_spec, any_spec],
+        in_specs=[pl.BlockSpec(memory_space=pltpu.HBM)] * 2,
         out_specs=(any_spec, pl.BlockSpec(memory_space=pltpu.VMEM)),
         scratch_shapes=[
+            pltpu.VMEM((ROWS, cells), jnp.float32), flat(CORES),
             flat(5), flat(), flat(3, M), flat(), flat(2, M), flat(), flat(2, M),
             pltpu.VMEM((SWEEPS, ROWS, LANES), jnp.float32),
-            pltpu.VMEM((nz * CORES, ROWS, LANES), jnp.float32),
+            pltpu.VMEM((nz, ROWS, LANES), jnp.float32),
             pltpu.VMEM((ny, ROWS, LANES), jnp.float32),
-            pltpu.VMEM((M, ROWS, LANES), jnp.float32),
-            dma((tiles + 2,)), dma((5, tiles + 2)), dma((5,)), dma((CORES, M)), dma((CORES, M)),
-            dma((nz * CORES,)), dma((nz * CORES,)), dma((ny,)), dma((ny,)), dma((M,)), dma((M,)),
+            pltpu.VMEM((M * CORES, ROWS, LANES), jnp.float32),
+            dma((1,)), dma((tiles + 2,)), dma((5, tiles + 2)), dma((CORES, tiles + 2)), dma((9,)),
+            dma((CORES, M)), dma((CORES, M)),
+            dma((nz,)), dma((nz,)), dma((ny,)), dma((ny,)), dma((M * CORES,)), dma((M * CORES,)),
         ],
         compiler_params=pltpu.CompilerParams(
             collective_id=0, has_side_effects=True, vmem_limit_bytes=48 * 2**20

time: 49.8 us -> 46.2 us (0.928)
  Pallas kernels: 45.6 us -> 41.9 us
    pallas_call x1, Pallas kernels: 45.6 us -> 41.9 us  [body(): pl.pallas_call(functools.partial(kernel, (ny, nz, cells, mean_count)), ou...]
where the time goes in v2:
time: 46.2 us; the launch traced here: 46 us
  Pallas kernels  41.9 us (91%)
  local copies, waits for them, and re-layouts  3.48 us (8%)
  between operations  0.65 us (1%)
    pallas_call x1, Pallas kernels, body(): pl.pallas_call(functools.partial(kernel, (ny, nz, cells, mean_count)), ou...  41.9 us
    unnamed x4, local copies, waits for them, and re-layouts  3.48 us

profile of v2, /device:TPU:1, one launch (start us, length us, event | category | flops | bytes accessed | tf_op | source)
XLA Modules:
  0.0 46.0 jit_solution(2457725405248256460)
XLA Ops:
  0.6 0.0 copy-start
  0.6 1.6 %copy-done = f32[1,32,16384]{2,1,0:T(8,128)S(1)} copy-done((f32[1,32,16384]{2,1,0:T(8,128)S(1)}, f32[1,32,16384]{2,1,0:T(8,128)}, u32[]{:S(2)}) %copy-start) | copy-done | bytes 2097176
  2.2 41.9 %sdc.1 = (f32[1,1,32,16384]{3,2,1,0:T(8,128)S(1)}, f32[3,32]{1,0:T(4,128)S(1)}) custom-call(f32[1,32,16384]{2,1,0:T(8,128)S(1)} %copy-done, f32[32,16384]{1,0:T(8,128)} %cp_ref.1), custom_call_target="tpu_custom_call" | custom-call | tf_op jit(solution)/shard_map/sdc/pallas_call | solution.py:434
  44.1 1.3 %copy.6 = f32[1,1,32,16384]{3,2,1,0:T(8,128)} copy(f32[1,1,32,16384]{3,2,1,0:T(8,128)S(1)} %get-tuple-element.4) | data formatting | bytes 4194304
  45.5 0.6 %copy.7 = f32[3,32]{1,0:T(4,128)} copy(f32[3,32]{1,0:T(4,128)S(1)} %get-tuple-element.5) | data formatting | bytes 768
Async XLA Ops:
  0.6 1.6 %copy-start = (f32[1,32,16384]{2,1,0:T(8,128)S(1)}, f32[1,32,16384]{2,1,0:T(8,128)}, u32[]{:S(2)}) copy-start(f32[1,32,16384]{2,1,0:T(8,128)} %ss_ref.1) | copy-start | bytes 6291460

commit v3 on v2

--- a/solution.py
+++ b/solution.py
@@ -72,8 +72,8 @@
 ROW_SUMS = [sum(row) for row in WEIGHTS]
 
 
-DIRECT = 5
-LEAD = 5
+LAG = 3
+AHEAD = 3
 
 
 def kernel(sizes, ss_ref, cp_ref, out_ref, res_ref, own, transit, buf, cbuf, u1, e1, u2, e2, rbuf, acc, st1, st2, st3,
@@ -140,21 +140,13 @@
         remote(own.at[:, cols(start, count)], buf.at[3 + core, :, cols(q, count)],
                zsend.at[4], rsem.at[3 + core, a], dev(chip, 1 - core), node).start()
 
-    def direct_set(a):
-        @pl.when(far_source)
-        def _():
-            for which in range(CORES):
-                start, q, count = source(which, a)
-                remote(own.at[:, cols(start, count)], buf.at[0, :, cols(q, count)],
-                       zsend.at[2 + which], rsem.at[0, a], dev(chip + 2, which), node).start()
-
     def first_leg(a):
         @pl.when(far_source)
         def _():
             for which in range(CORES):
                 start, q, count = source(which, a)
                 remote(own.at[:, cols(start, count)], transit.at[which, :, cols(q, count)],
-                       zsend.at[5 + which], tsem.at[which, a], dev(middle, 0), node).start()
+                       zsend.at[2 + which], tsem.at[which, a], dev(middle, 0), node).start()
 
     def second_leg(a):
         for which in range(CORES):
@@ -162,7 +154,7 @@
             view = transit.at[which, :, cols(q, count)]
             pltpu.make_async_copy(view, view, tsem.at[which, a]).wait()
             remote(view, buf.at[0, :, cols(q, count)],
-                   zsend.at[7 + which], rsem.at[0, a], dev(target, which), node).start()
+                   zsend.at[5 + which], rsem.at[0, a], dev(target, which), node).start()
 
     def wait_set(a):
         _, q, count = source(core, a)
@@ -180,9 +172,12 @@
             arrived(1)
             arrived(2)
 
+    def wait_far_set(a):
         @pl.when(far_target)
         def _():
-            arrived(0)
+            _, q, count = source(core, a)
+            view = buf.at[0, :, cols(q, count)]
+            pltpu.make_async_copy(view, view, rsem.at[0, a]).wait()
 
     fetch = pltpu.make_async_copy(ss_ref.at[0, rows, :], own, wsem.at[0])
     fetch.start()
@@ -205,8 +200,6 @@
     for cond, count, hello in (
         (has_next, 2, lambda: both(chip + 1)),
         (has_before, 2, lambda: both(chip - 1)),
-        (far_source, 2, lambda: both(chip + 2)),
-        (far_target, 1, lambda: greet(dev(chip - 2, 1), node)),
         (far_source, 1, lambda: greet(dev(middle, 0), node)),
         (far_middle, 1, lambda: greet(dev(source_chip, 1), node)),
         (far_middle, 2, lambda: both(target)),
@@ -226,18 +219,13 @@
     pl.semaphore_wait(barrier, greeted + always)
     fetch.wait()
 
-    direct_set(0)
     near_set(0)
-
-    @pl.loop(1, DIRECT + 1)
+    first_leg(0)
+
+    @pl.loop(1, sets)
     def _(a):
-        direct_set(a)
         near_set(a)
-
-    @pl.loop(DIRECT + 1, sets)
-    def _(a):
         first_leg(a)
-        near_set(a)
 
     acc[...] = jnp.zeros_like(acc)
     first = chip == 0
@@ -263,18 +251,19 @@
         return twice, defect
 
     def add_up(k, q, total):
-        parts = []
+        whole_tile = None
         for t in range(TILE):
             mine = jnp.logical_and(q + t >= PAD, q + t < PAD + half)
             part = total[:, t * LANES:(t + 1) * LANES]
-            parts.append(jnp.where(mine, part, jnp.zeros_like(part)))
-        acc[k] += (parts[0] + parts[1]) + (parts[2] + parts[3])
-
-    def start_sweep(q):
+            part = jnp.where(mine, part, jnp.zeros_like(part))
+            whole_tile = part if whole_tile is None else whole_tile + part
+        acc[k] += whole_tile
+
+    def start_sweep(q, slices):
         cw = cbuf[:, cols(q - 1, TILE + 2)]
         here = cols(q, TILE)
         total = None
-        for n in range(1, 5):
+        for n in slices:
             u, square, g, f = force(buf.at[n], q, cw)
             before = buf[n - 1, :, here]
             if n == 3:
@@ -291,14 +280,15 @@
                     u1[n - 2, m, :, here] = new
                 if n >= 3:
                     total = defect * defect if total is None else total + defect * defect
-        add_up(0, q, total)
-
-    def later_sweep(k, q):
+        if total is not None:
+            add_up(0, q, total)
+
+    def later_sweep(k, q, slices):
         cw = cbuf[:, cols(q - 1, TILE + 2)]
         here = cols(q, TILE)
         total = None
         old = u1 if k == 1 else u2
-        for n in range(2 if k == 1 else 3, 5):
+        for n in slices:
             slot = n - 2 if k == 1 else n - 3
             parts = [force(old.at[slot, m], q, cw) for m in range(M)]
             if n == 2:
@@ -323,42 +313,59 @@
                     rbuf[n - 3, m, :, here] = new
                 if n >= 3:
                     total = defect * defect if total is None else total + defect * defect
-        add_up(k, q, total)
-
-    def send_out(i):
-        q = PAD + TILE * i
+        if total is not None:
+            add_up(k, q, total)
+
+    def send_out(which, i):
         place = cols(core * half + TILE * i, TILE)
         for away in range(M):
             to_node = lax.rem(node + away, M)
-            for other in range(CORES):
-                which = core if other == 0 else 1 - core
-                src = rbuf.at[which, to_node, :, cols(q, TILE)]
-                dst = out_ref.at[0, 0, rows, place]
-                if away == 0 and other == 0:
-                    pltpu.make_async_copy(src, dst, osend.at[0, 0]).start()
-                else:
-                    remote(src, dst, osend.at[other, away], orecv.at[other, away],
-                           dev(chip, which), to_node).start()
+            src = rbuf.at[which, to_node, :, cols(PAD + TILE * i, TILE)]
+            dst = out_ref.at[0, 0, rows, place]
+            out = remote(src, dst, osend.at[which, away], orecv.at[core, away], dev(chip, which), to_node)
+            if away:
+                out.start()
+            else:
+                pl.when(core != which)(out.start)
+                pl.when(core == which)(pltpu.make_async_copy(src, dst, osend.at[which, 0]).start)
 
     wait_set(0)
 
-    @pl.loop(0, tiles + 1)
+    @pl.when(far_middle)
+    def _():
+        second_leg(0)
+
+        @pl.loop(1, AHEAD)
+        def _(a):
+            second_leg(a)
+
+    wait_far_set(0)
+
+    @pl.loop(0, tiles + 1 + LAG)
     def _(step):
-        i = step - 1
-
-        @pl.when(jnp.logical_and(far_middle, step + LEAD + 1 < sets))
-        def _():
-            second_leg(step + LEAD + 1)
-
-        wait_set(step + 1)
-        q = PAD + TILE * i
-        start_sweep(q + 2)
-        later_sweep(1, q + 1)
-        later_sweep(2, q)
-
-        @pl.when(step > 0)
-        def _():
-            send_out(i)
+        @pl.when(jnp.logical_and(far_middle, step + AHEAD < sets))
+        def _():
+            second_leg(step + AHEAD)
+
+        @pl.when(step <= tiles)
+        def _():
+            i = step - 1
+            wait_set(step + 1)
+            q = PAD + TILE * i
+            start_sweep(q + 2, (4, 3, 2))
+            later_sweep(1, q + 1, (4, 3))
+            later_sweep(2, q, (4,))
+            pl.when(i >= 0)(lambda: send_out(1, i))
+
+        @pl.when(step >= LAG)
+        def _():
+            i = step - 1 - LAG
+            wait_far_set(i + 2)
+            q = PAD + TILE * i
+            start_sweep(q + 2, (1,))
+            later_sweep(1, q + 1, (2,))
+            later_sweep(2, q, (3,))
+            pl.when(i >= 0)(lambda: send_out(0, i))
 
     lane = lax.broadcasted_iota(jnp.int32, (ROWS, LANES), 1)
     sums = jnp.zeros((ROWS, LANES), jnp.float32)
@@ -405,20 +412,24 @@
     @pl.when(far_source)
     def _():
         for which in range(CORES):
-            ended(2 + which, 1 + TILE * DIRECT)
-            ended(5 + which, TILE * (sets - 1 - DIRECT))
+            ended(2 + which, 1 + TILE * (sets - 1))
 
     @pl.when(far_middle)
     def _():
         for which in range(CORES):
-            ended(7 + which, TILE * (sets - 1 - DIRECT))
+            ended(5 + which, 1 + TILE * (sets - 1))
 
     made = rbuf.at[0, 0, :, cols(0, half)]
+
+    def drained(sem):
+        pltpu.make_async_copy(made, made, sem).wait()
+
     for away in range(M):
-        for other in range(CORES):
-            pltpu.make_async_copy(made, made, osend.at[other, away]).wait()
-            if away or other:
-                pltpu.make_async_copy(made, made, orecv.at[other, away]).wait()
+        for which in range(CORES):
+            drained(osend.at[which, away])
+            if away:
+                drained(orecv.at[which, away])
+    drained(orecv.at[1 - core, 0])
 
 
 def body(sizes, slice_starts, coupling):
@@ -446,7 +457,7 @@
             pltpu.VMEM((nz, ROWS, LANES), jnp.float32),
             pltpu.VMEM((ny, ROWS, LANES), jnp.float32),
             pltpu.VMEM((M * CORES, ROWS, LANES), jnp.float32),
-            dma((1,)), dma((tiles + 2,)), dma((5, tiles + 2)), dma((CORES, tiles + 2)), dma((9,)),
+            dma((1,)), dma((tiles + 2,)), dma((5, tiles + 2)), dma((CORES, tiles + 2)), dma((7,)),
             dma((CORES, M)), dma((CORES, M)),
             dma((nz,)), dma((nz,)), dma((ny,)), dma((ny,)), dma((M * CORES,)), dma((M * CORES,)),
         ],

time: 46.2 us -> 51 us (1.10)
  Pallas kernels: 41.9 us -> 46.7 us
    pallas_call x1, Pallas kernels: 41.9 us -> 46.7 us  [body(): pl.pallas_call(functools.partial(kernel, (ny, nz, cells, mean_count)), ou...]
where the time goes in v3:
time: 51 us; the launch traced here: 50.8 us
  Pallas kernels  46.7 us (92%)
  local copies, waits for them, and re-layouts  3.48 us (7%)
  between operations  0.65 us (1%)
    pallas_call x1, Pallas kernels, body(): pl.pallas_call(functools.partial(kernel, (ny, nz, cells, mean_count)), ou...  46.7 us
    unnamed x4, local copies, waits for them, and re-layouts  3.48 us

profile of v3, /device:TPU:1, one launch (start us, length us, event | category | flops | bytes accessed | tf_op | source)
XLA Modules:
  0.0 50.8 jit_solution(6448413270504566946)
XLA Ops:
  0.6 0.0 copy-start
  0.6 1.6 %copy-done = f32[1,32,16384]{2,1,0:T(8,128)S(1)} copy-done((f32[1,32,16384]{2,1,0:T(8,128)S(1)}, f32[1,32,16384]{2,1,0:T(8,128)}, u32[]{:S(2)}) %copy-start) | copy-done | bytes 2097176
  2.2 46.7 %sdc.1 = (f32[1,1,32,16384]{3,2,1,0:T(8,128)S(1)}, f32[3,32]{1,0:T(4,128)S(1)}) custom-call(f32[1,32,16384]{2,1,0:T(8,128)S(1)} %copy-done, f32[32,16384]{1,0:T(8,128)} %cp_ref.1), custom_call_target="tpu_custom_call" | custom-call | tf_op jit(solution)/shard_map/sdc/pallas_call | solution.py:445
  48.9 1.3 %copy.6 = f32[1,1,32,16384]{3,2,1,0:T(8,128)} copy(f32[1,1,32,16384]{3,2,1,0:T(8,128)S(1)} %get-tuple-element.4) | data formatting | bytes 4194304
  50.2 0.6 %copy.7 = f32[3,32]{1,0:T(4,128)} copy(f32[3,32]{1,0:T(4,128)S(1)} %get-tuple-element.5) | data formatting | bytes 768
Async XLA Ops:
  0.6 1.6 %copy-start = (f32[1,32,16384]{2,1,0:T(8,128)S(1)}, f32[1,32,16384]{2,1,0:T(8,128)}, u32[]{:S(2)}) copy-start(f32[1,32,16384]{2,1,0:T(8,128)} %ss_ref.1) | copy-start | bytes 6291460

commit v4 on v3

--- a/solution.py
+++ b/solution.py
@@ -13,8 +13,9 @@
 CORES = 2
 LANES = 128
 ROWS = 8
+SUB = 2
 TILE = 4
-PAD = 5
+PAD = TILE + 1
 time_step = 0.5
 log_floor = 0.05
 
@@ -76,7 +77,17 @@
 AHEAD = 3
 
 
-def kernel(sizes, ss_ref, cp_ref, out_ref, res_ref, own, transit, buf, cbuf, u1, e1, u2, e2, rbuf, acc, st1, st2, st3,
+SS = 0
+CP, CL, CS = 5, 6, 7
+U1 = 8
+E1 = U1 + 3 * M * 3
+U2 = E1 + 1
+E2 = U2 + 2 * M * 3
+OUT = E2 + 1
+PLACES = OUT + 2 * M
+
+
+def kernel(sizes, ss_ref, cp_ref, out_ref, res_ref, own, transit, arena, acc, st1, st2, st3,
            wsem, csem, rsem, tsem, zsend, osend, orecv, s1s, s1r, s2s, s2r, s3s, s3r):
     ny, nz, cells, mean_count = sizes
     half = cells // LANES // CORES
@@ -123,9 +134,9 @@
 
     def local_set(a):
         start, q, count = source(core, a)
-        pltpu.make_async_copy(cp_ref.at[rows, cols(start, count)], cbuf.at[:, cols(q, count)], csem.at[a]).start()
+        pltpu.make_async_copy(cp_ref.at[rows, cols(start, count)], arena.at[CP, :, cols(q, count)], csem.at[a]).start()
         pltpu.make_async_copy(
-            ss_ref.at[0, rows, cols(start, count)], buf.at[3 + core, :, cols(q, count)], rsem.at[3 + core, a]
+            ss_ref.at[0, rows, cols(start, count)], arena.at[3 + core, :, cols(q, count)], rsem.at[3 + core, a]
         ).start()
 
     def near_set(a):
@@ -133,11 +144,11 @@
         def _():
             for which in range(CORES):
                 start, q, count = source(which, a)
-                remote(own.at[:, cols(start, count)], buf.at[1 + core, :, cols(q, count)],
+                remote(own.at[:, cols(start, count)], arena.at[1 + core, :, cols(q, count)],
                        zsend.at[which], rsem.at[1 + core, a], dev(chip + 1, which), node).start()
 
         start, q, count = source(1 - core, a)
-        remote(own.at[:, cols(start, count)], buf.at[3 + core, :, cols(q, count)],
+        remote(own.at[:, cols(start, count)], arena.at[3 + core, :, cols(q, count)],
                zsend.at[4], rsem.at[3 + core, a], dev(chip, 1 - core), node).start()
 
     def first_leg(a):
@@ -153,15 +164,15 @@
             _, q, count = source(which, a)
             view = transit.at[which, :, cols(q, count)]
             pltpu.make_async_copy(view, view, tsem.at[which, a]).wait()
-            remote(view, buf.at[0, :, cols(q, count)],
+            remote(view, arena.at[0, :, cols(q, count)],
                    zsend.at[5 + which], rsem.at[0, a], dev(target, which), node).start()
 
     def wait_set(a):
         _, q, count = source(core, a)
-        pltpu.make_async_copy(cbuf.at[:, cols(q, count)], cbuf.at[:, cols(q, count)], csem.at[a]).wait()
+        pltpu.make_async_copy(arena.at[CP, :, cols(q, count)], arena.at[CP, :, cols(q, count)], csem.at[a]).wait()
 
         def arrived(n):
-            view = buf.at[n, :, cols(q, count)]
+            view = arena.at[n, :, cols(q, count)]
             pltpu.make_async_copy(view, view, rsem.at[n, a]).wait()
 
         arrived(3)
@@ -176,7 +187,7 @@
         @pl.when(far_target)
         def _():
             _, q, count = source(core, a)
-            view = buf.at[0, :, cols(q, count)]
+            view = arena.at[0, :, cols(q, count)]
             pltpu.make_async_copy(view, view, rsem.at[0, a]).wait()
 
     fetch = pltpu.make_async_copy(ss_ref.at[0, rows, :], own, wsem.at[0])
@@ -230,97 +241,159 @@
     acc[...] = jnp.zeros_like(acc)
     first = chip == 0
     second = chip == 1
-    width = TILE * LANES
-
-    def force(ref, q, cw):
-        x = ref[:, cols(q - 1, TILE + 2)]
-        flux = cw * (pltpu.roll(x, (TILE + 2) * LANES - 1, axis=1) - x)
-        spread = flux - pltpu.roll(flux, 1, axis=1)
-        u = x[:, LANES:LANES + width]
-        square = u * u
-        g = u - u * square
-        return u, square, g, spread[:, LANES:LANES + width] + g
-
-    def newton(u, square, g, base, m):
+    width = SUB * LANES
+    lane = lax.broadcasted_iota(jnp.int32, (ROWS, width), 1) % LANES
+    low = lane == 0
+    high = lane == LANES - 1
+
+    def load(v, place, q, count=SUB):
+        return v[place, :, cols(q, count)]
+
+    def piece(value, t):
+        return value[:, t * LANES:(t + 1) * LANES]
+
+    def rolled(v, place, q, count, by):
+        return jnp.concatenate([pltpu.roll(load(v, place, q + t, 1), by, axis=1) for t in range(count)], axis=1)
+
+    def pick_right(turned):
+        return jnp.where(high, turned[:, LANES:], turned[:, :width])
+
+    def pick_left(turned):
+        return jnp.where(low, turned[:, :width], turned[:, LANES:])
+
+    def force(u, square, right, left, parts):
+        c, cl, cs = parts
+        return c * right + cl * left + u * (cs - square)
+
+    def newton(u, square3, defect, target, m):
         a = IMPLICIT[m]
-        defect = base - u
-        target = base - a * g
-        once = u + defect / ((1.0 - a) + (3.0 * a) * square)
+        once = u + defect / ((1.0 - a) + square3)
         square = once * once
-        twice = (target + (2.0 * a) * square * once) / ((1.0 - a) + (3.0 * a) * square)
-        return twice, defect
+        return (target + (2.0 * a) * square * once) / ((1.0 - a) + (3.0 * a) * square)
+
+    def keep(v, place, q, new):
+        for t in range(SUB):
+            part = piece(new, t)
+            v[place, :, cols(q + t, 1)] = part
+            v[place + 1, :, cols(q + t, 1)] = pltpu.roll(part, LANES - 1, axis=1)
+            v[place + 2, :, cols(q + t, 1)] = pltpu.roll(part, 1, axis=1)
 
     def add_up(k, q, total):
         whole_tile = None
-        for t in range(TILE):
+        for t in range(SUB):
             mine = jnp.logical_and(q + t >= PAD, q + t < PAD + half)
-            part = total[:, t * LANES:(t + 1) * LANES]
-            part = jnp.where(mine, part, jnp.zeros_like(part))
+            part = jnp.where(mine, piece(total, t), jnp.zeros((ROWS, LANES), jnp.float32))
             whole_tile = part if whole_tile is None else whole_tile + part
         acc[k] += whole_tile
 
-    def start_sweep(q, slices):
-        cw = cbuf[:, cols(q - 1, TILE + 2)]
-        here = cols(q, TILE)
+    def start_sweep(v, first_col, q, slices):
+        here = cols(q, SUB)
+        c = load(v, CP, q)
+        if 1 in slices:
+            parts = (c, load(v, CL, q), load(v, CS, q))
+        else:
+            cl = pick_left(rolled(v, CP, q - 1, SUB + 1, 1))
+            cs = 1.0 - (c + cl)
+            v[CL, :, here] = cl
+            v[CS, :, here] = cs
+            parts = (c, cl, cs)
         total = None
         for n in slices:
-            u, square, g, f = force(buf.at[n], q, cw)
-            before = buf[n - 1, :, here]
+            u = load(v, SS + n, q)
+            square = u * u
+            f = force(u, square, pick_right(rolled(v, SS + n, q, SUB + 1, LANES - 1)),
+                      pick_left(rolled(v, SS + n, q - 1, SUB + 1, 1)), parts)
+            before = load(v, SS + n - 1, q)
             if n == 3:
                 before = jnp.where(first, u, before)
             if n == 1:
                 before = jnp.where(second, u, before)
+            pull = f - 0.25 * (u - u * square)
+            gap = before - u
             for m in range(M):
                 if n == 1 and m < M - 1:
                     continue
-                new, defect = newton(u, square, g, before + ROW_SUMS[m] * f, m)
+                defect = gap + ROW_SUMS[m] * f
+                new = newton(u, (3.0 * IMPLICIT[m]) * square, defect, before + ROW_SUMS[m] * pull, m)
                 if n == 1:
-                    e1[:, here] = new
+                    v[E1, :, here] = new
                 else:
-                    u1[n - 2, m, :, here] = new
+                    keep(v, U1 + ((n - 2) * M + m) * 3, q, new)
                 if n >= 3:
                     total = defect * defect if total is None else total + defect * defect
         if total is not None:
-            add_up(0, q, total)
-
-    def later_sweep(k, q, slices):
-        cw = cbuf[:, cols(q - 1, TILE + 2)]
-        here = cols(q, TILE)
+            add_up(0, first_col + q, total)
+
+    def later_sweep(v, first_col, k, q, slices):
+        here = cols(q, SUB)
+        parts = (load(v, CP, q), load(v, CL, q), load(v, CS, q))
         total = None
-        old = u1 if k == 1 else u2
         for n in slices:
-            slot = n - 2 if k == 1 else n - 3
-            parts = [force(old.at[slot, m], q, cw) for m in range(M)]
+            at = U1 + (n - 2) * M * 3 if k == 1 else U2 + (n - 3) * M * 3
+            us, squares, forces = [], [], []
+            for m in range(M):
+                u = load(v, at + 3 * m, q)
+                square = u * u
+                right = pick_right(load(v, at + 3 * m + 1, q, SUB + 1))
+                left = pick_left(load(v, at + 3 * m + 2, q - 1, SUB + 1))
+                us.append(u)
+                squares.append(square)
+                forces.append(force(u, square, right, left, parts))
             if n == 2:
-                before = e1[:, here]
+                before = load(v, E1, q)
             elif n == 3:
-                before = u1[0, M - 1, :, here] if k == 1 else e2[:, here]
-                before = jnp.where(first, buf[3, :, here], before)
+                before = load(v, U1 + (M - 1) * 3 if k == 1 else E2, q)
+                before = jnp.where(first, load(v, SS + 3, q), before)
             else:
-                before = old[slot - 1, M - 1, :, here]
+                before = load(v, at - 3, q)
             for m in range(M):
                 if n == 2 and m < M - 1:
                     continue
                 base = before
                 for j in range(M):
-                    base = base + WEIGHTS[m][j] * parts[j][3]
-                new, defect = newton(parts[m][0], parts[m][1], parts[m][2], base, m)
+                    base = base + WEIGHTS[m][j] * forces[j]
+                a = IMPLICIT[m]
+                defect = base - us[m]
+                scaled = a * squares[m]
+                target = defect + us[m] * ((1.0 - a) + scaled)
+                new = newton(us[m], 3.0 * scaled, defect, target, m)
                 if n == 2:
-                    e2[:, here] = new
+                    v[E2, :, here] = new
                 elif k == 1:
-                    u2[n - 3, m, :, here] = new
+                    keep(v, U2 + ((n - 3) * M + m) * 3, q, new)
                 else:
-                    rbuf[n - 3, m, :, here] = new
+                    v[OUT + (n - 3) * M + m, :, here] = new
                 if n >= 3:
                     total = defect * defect if total is None else total + defect * defect
         if total is not None:
-            add_up(k, q, total)
+            add_up(k, first_col + q, total)
+
+    def window(step):
+        return arena.at[:, :, cols(step * TILE, TILE + 6)], step * TILE
+
+    def main_part(step):
+        v, at = window(step)
+        for g in range(0, TILE, SUB):
+            start_sweep(v, at, 3 + g, (4, 3, 2))
+        for g in range(0, TILE, SUB):
+            later_sweep(v, at, 1, 2 + g, (4, 3))
+        for g in range(0, TILE, SUB):
+            later_sweep(v, at, 2, 1 + g, (4,))
+
+    def lagging_part(step):
+        v, at = window(step)
+        for g in range(0, TILE, SUB):
+            start_sweep(v, at, 3 + g, (1,))
+        for g in range(0, TILE, SUB):
+            later_sweep(v, at, 1, 2 + g, (2,))
+        for g in range(0, TILE, SUB):
+            later_sweep(v, at, 2, 1 + g, (3,))
 
     def send_out(which, i):
         place = cols(core * half + TILE * i, TILE)
         for away in range(M):
             to_node = lax.rem(node + away, M)
-            src = rbuf.at[which, to_node, :, cols(PAD + TILE * i, TILE)]
+            src = arena.at[OUT + which * M + to_node, :, cols(PAD + TILE * i, TILE)]
             dst = out_ref.at[0, 0, rows, place]
             out = remote(src, dst, osend.at[which, away], orecv.at[core, away], dev(chip, which), to_node)
             if away:
@@ -351,26 +424,20 @@
         def _():
             i = step - 1
             wait_set(step + 1)
-            q = PAD + TILE * i
-            start_sweep(q + 2, (4, 3, 2))
-            later_sweep(1, q + 1, (4, 3))
-            later_sweep(2, q, (4,))
+            main_part(step)
             pl.when(i >= 0)(lambda: send_out(1, i))
 
         @pl.when(step >= LAG)
         def _():
             i = step - 1 - LAG
             wait_far_set(i + 2)
-            q = PAD + TILE * i
-            start_sweep(q + 2, (1,))
-            later_sweep(1, q + 1, (2,))
-            later_sweep(2, q, (3,))
+            lagging_part(step - LAG)
             pl.when(i >= 0)(lambda: send_out(0, i))
 
-    lane = lax.broadcasted_iota(jnp.int32, (ROWS, LANES), 1)
+    column = lax.broadcasted_iota(jnp.int32, (ROWS, LANES), 1)
     sums = jnp.zeros((ROWS, LANES), jnp.float32)
     for k in range(SWEEPS):
-        sums = jnp.where(lane == k, jnp.sum(acc[k], axis=1, keepdims=True), sums)
+        sums = jnp.where(column == k, jnp.sum(acc[k], axis=1, keepdims=True), sums)
 
     def swap(store, mine, value, peers, send, recv):
         store[mine] = value
@@ -419,7 +486,7 @@
         for which in range(CORES):
             ended(5 + which, 1 + TILE * (sets - 1))
 
-    made = rbuf.at[0, 0, :, cols(0, half)]
+    made = arena.at[OUT, :, cols(0, half)]
 
     def drained(sem):
         pltpu.make_async_copy(made, made, sem).wait()
@@ -437,7 +504,7 @@
     ny, nz = sizes
     half = cells // LANES // CORES
     tiles = half // TILE
-    span = half + PAD + TILE
+    span = half + 2 * TILE + 6
     mean_count = float(ny * nz * CORES * M * cells)
     flat = lambda *lead: pltpu.VMEM(lead + (ROWS, span * LANES), jnp.float32)
     dma = pltpu.SemaphoreType.DMA
@@ -451,8 +518,7 @@
         in_specs=[pl.BlockSpec(memory_space=pltpu.HBM)] * 2,
         out_specs=(any_spec, pl.BlockSpec(memory_space=pltpu.VMEM)),
         scratch_shapes=[
-            pltpu.VMEM((ROWS, cells), jnp.float32), flat(CORES),
-            flat(5), flat(), flat(3, M), flat(), flat(2, M), flat(), flat(2, M),
+            pltpu.VMEM((ROWS, cells), jnp.float32), flat(CORES), flat(PLACES),
             pltpu.VMEM((SWEEPS, ROWS, LANES), jnp.float32),
             pltpu.VMEM((nz, ROWS, LANES), jnp.float32),
             pltpu.VMEM((ny, ROWS, LANES), jnp.float32),

time: 51 us -> 44.8 us (0.88)
  Pallas kernels: 46.7 us -> 40.5 us
    pallas_call x1, Pallas kernels: 46.7 us -> 40.5 us  [body(): pl.pallas_call(functools.partial(kernel, (ny, nz, cells, mean_count)), ou...]
where the time goes in v4:
time: 44.8 us; the launch traced here: 44.7 us
  Pallas kernels  40.5 us (90%)
  local copies, waits for them, and re-layouts  3.48 us (8%)
  between operations  0.65 us (1%)
    pallas_call x1, Pallas kernels, body(): pl.pallas_call(functools.partial(kernel, (ny, nz, cells, mean_count)), ou...  40.5 us
    unnamed x4, local copies, waits for them, and re-layouts  3.48 us

profile of v4, /device:TPU:1, one launch (start us, length us, event | category | flops | bytes accessed | tf_op | source)
XLA Modules:
  0.0 44.7 jit_solution(15190470972593765039)
XLA Ops:
  0.6 0.0 copy-start
  0.6 1.6 %copy-done = f32[1,32,16384]{2,1,0:T(8,128)S(1)} copy-done((f32[1,32,16384]{2,1,0:T(8,128)S(1)}, f32[1,32,16384]{2,1,0:T(8,128)}, u32[]{:S(2)}) %copy-start) | copy-done | bytes 2097176
  2.2 40.5 %sdc.1 = (f32[1,1,32,16384]{3,2,1,0:T(8,128)S(1)}, f32[3,32]{1,0:T(4,128)S(1)}) custom-call(f32[1,32,16384]{2,1,0:T(8,128)S(1)} %copy-done, f32[32,16384]{1,0:T(8,128)} %cp_ref.1), custom_call_target="tpu_custom_call" | custom-call | tf_op jit(solution)/shard_map/sdc/pallas_call | solution.py:512
  42.8 1.3 %copy.6 = f32[1,1,32,16384]{3,2,1,0:T(8,128)} copy(f32[1,1,32,16384]{3,2,1,0:T(8,128)S(1)} %get-tuple-element.4) | data formatting | bytes 4194304
  44.1 0.6 %copy.7 = f32[3,32]{1,0:T(4,128)} copy(f32[3,32]{1,0:T(4,128)S(1)} %get-tuple-element.5) | data formatting | bytes 768
Async XLA Ops:
  0.6 1.6 %copy-start = (f32[1,32,16384]{2,1,0:T(8,128)S(1)}, f32[1,32,16384]{2,1,0:T(8,128)}, u32[]{:S(2)}) copy-start(f32[1,32,16384]{2,1,0:T(8,128)} %ss_ref.1) | copy-start | bytes 6291460

commit v5 on v4

--- a/solution.py
+++ b/solution.py
@@ -87,9 +87,9 @@
 PLACES = OUT + 2 * M
 
 
-def kernel(sizes, ss_ref, cp_ref, out_ref, res_ref, own, transit, arena, acc, st1, st2, st3,
+def kernel(sizes, ss_ref, cp_ref, out_ref, sums_ref, own, transit, arena, acc, st1, st2, st3,
            wsem, csem, rsem, tsem, zsend, osend, orecv, s1s, s1r, s2s, s2r, s3s, s3r):
-    ny, nz, cells, mean_count = sizes
+    ny, nz, cells = sizes
     half = cells // LANES // CORES
     tiles = half // TILE
     whole = cells // LANES
@@ -130,7 +130,12 @@
     def source(which, a):
         if isinstance(a, int) and a == 0:
             return lax.rem(half * which + whole - 1, whole), PAD - 1, 1
-        return lax.rem(half * which + TILE * (a - 1), whole), PAD + TILE * (a - 1), TILE
+        count = 1 if isinstance(a, int) and a == sets - 1 else TILE
+        return lax.rem(half * which + TILE * (a - 1), whole), PAD + TILE * (a - 1), count
+
+    def each_set(a, what):
+        pl.when(a < sets - 1)(lambda: what(a))
+        pl.when(a == sets - 1)(lambda: what(sets - 1))
 
     def local_set(a):
         start, q, count = source(core, a)
@@ -194,9 +199,11 @@
     fetch.start()
     local_set(0)
 
-    @pl.loop(1, sets)
+    @pl.loop(1, sets - 1)
     def _(a):
         local_set(a)
+
+    local_set(sets - 1)
 
     barrier = pltpu.get_barrier_semaphore()
 
@@ -233,10 +240,13 @@
     near_set(0)
     first_leg(0)
 
-    @pl.loop(1, sets)
+    @pl.loop(1, sets - 1)
     def _(a):
         near_set(a)
         first_leg(a)
+
+    near_set(sets - 1)
+    first_leg(sets - 1)
 
     acc[...] = jnp.zeros_like(acc)
     first = chip == 0
@@ -416,28 +426,31 @@
 
     @pl.loop(0, tiles + 1 + LAG)
     def _(step):
-        @pl.when(jnp.logical_and(far_middle, step + AHEAD < sets))
-        def _():
-            second_leg(step + AHEAD)
+        @pl.when(far_middle)
+        def _():
+            each_set(step + AHEAD, second_leg)
 
         @pl.when(step <= tiles)
         def _():
             i = step - 1
-            wait_set(step + 1)
+            each_set(step + 1, wait_set)
             main_part(step)
             pl.when(i >= 0)(lambda: send_out(1, i))
 
         @pl.when(step >= LAG)
         def _():
             i = step - 1 - LAG
-            wait_far_set(i + 2)
+            each_set(i + 2, wait_far_set)
             lagging_part(step - LAG)
             pl.when(i >= 0)(lambda: send_out(0, i))
 
+    row = lax.broadcasted_iota(jnp.int32, (ROWS, LANES), 0)
     column = lax.broadcasted_iota(jnp.int32, (ROWS, LANES), 1)
+    place = column == node * ROWS + row
     sums = jnp.zeros((ROWS, LANES), jnp.float32)
     for k in range(SWEEPS):
-        sums = jnp.where(column == k, jnp.sum(acc[k], axis=1, keepdims=True), sums)
+        spread = jnp.where(place, jnp.sum(acc[k], axis=1, keepdims=True), 0.0)
+        sums = jnp.where(row == k, jnp.sum(spread, axis=0, keepdims=True), sums)
 
     def swap(store, mine, value, peers, send, recv):
         store[mine] = value
@@ -457,34 +470,31 @@
     me = node * CORES + core
     peers = [lax.rem(me + by, M * CORES) for by in range(1, M * CORES)]
     swap(st3, me, sums, [(dev(chip, lax.rem(p, CORES)), lax.div(p, CORES)) for p in peers], s3s, s3r)
-    table = jnp.concatenate(
-        [st3[CORES * m] + st3[CORES * m + 1] for m in range(M)]
-        + [jnp.zeros((LANES - M * ROWS, LANES), jnp.float32)],
-        axis=0,
-    )
-    table = jnp.log(log_floor + table.T / mean_count)
-    res_ref[...] = table[:SWEEPS, :M * ROWS]
+    sums = st3[0]
+    for slot in range(1, M * CORES):
+        sums = sums + st3[slot]
+    sums_ref[...] = sums
 
     def ended(flow, count):
         view = own.at[:, cols(0, count)]
         pltpu.make_async_copy(view, view, zsend.at[flow]).wait()
 
-    ended(4, 1 + TILE * (sets - 1))
+    ended(4, 2 + TILE * (sets - 2))
 
     @pl.when(has_next)
     def _():
-        ended(0, 1 + TILE * (sets - 1))
-        ended(1, 1 + TILE * (sets - 1))
+        ended(0, 2 + TILE * (sets - 2))
+        ended(1, 2 + TILE * (sets - 2))
 
     @pl.when(far_source)
     def _():
         for which in range(CORES):
-            ended(2 + which, 1 + TILE * (sets - 1))
+            ended(2 + which, 2 + TILE * (sets - 2))
 
     @pl.when(far_middle)
     def _():
         for which in range(CORES):
-            ended(5 + which, 1 + TILE * (sets - 1))
+            ended(5 + which, 2 + TILE * (sets - 2))
 
     made = arena.at[OUT, :, cols(0, half)]
 
@@ -497,6 +507,22 @@
             if away:
                 drained(orecv.at[which, away])
     drained(orecv.at[1 - core, 0])
+
+
+def finish(mean_count, made_ref, sums_ref, out_ref, log_ref, row, sem):
+    systems = made_ref.shape[2]
+    flows = []
+    for block in range(systems // ROWS):
+        rows = pl.ds(block * ROWS, ROWS)
+        flows.append(pltpu.make_async_copy(made_ref.at[0, 0, rows], out_ref.at[0, 0, rows], sem.at[block]))
+    for c in flows:
+        c.start()
+    row[...] = jnp.log(log_floor + sums_ref[...] / mean_count)[:SWEEPS, :systems]
+    last = pltpu.make_async_copy(row, log_ref, sem.at[systems // ROWS])
+    last.start()
+    for c in flows:
+        c.wait()
+    last.wait()
 
 
 def body(sizes, slice_starts, coupling):
@@ -509,12 +535,10 @@
     flat = lambda *lead: pltpu.VMEM(lead + (ROWS, span * LANES), jnp.float32)
     dma = pltpu.SemaphoreType.DMA
     any_spec = pl.BlockSpec(memory_space=pl.ANY)
-    return pl.pallas_call(
-        functools.partial(kernel, (ny, nz, cells, mean_count)),
-        out_shape=(
-            jax.ShapeDtypeStruct((1, 1, systems, cells), jnp.float32),
-            jax.ShapeDtypeStruct((SWEEPS, systems), jnp.float32),
-        ),
+    out = jax.ShapeDtypeStruct((1, 1, systems, cells), jnp.float32)
+    made, sums = pl.pallas_call(
+        functools.partial(kernel, (ny, nz, cells)),
+        out_shape=(out, jax.ShapeDtypeStruct((ROWS, LANES), jnp.float32)),
         in_specs=[pl.BlockSpec(memory_space=pltpu.HBM)] * 2,
         out_specs=(any_spec, pl.BlockSpec(memory_space=pltpu.VMEM)),
         scratch_shapes=[
@@ -528,10 +552,19 @@
             dma((nz,)), dma((nz,)), dma((ny,)), dma((ny,)), dma((M * CORES,)), dma((M * CORES,)),
         ],
         compiler_params=pltpu.CompilerParams(
-            collective_id=0, has_side_effects=True, vmem_limit_bytes=48 * 2**20
+            collective_id=0, has_side_effects=True, vmem_limit_bytes=51 * 2**20
         ),
         name="sdc",
     )(slice_starts, coupling)
+    return pl.pallas_call(
+        functools.partial(finish, mean_count),
+        out_shape=(out, jax.ShapeDtypeStruct((SWEEPS, systems), jnp.float32)),
+        in_specs=[any_spec, pl.BlockSpec(memory_space=pltpu.VMEM)],
+        out_specs=(pl.BlockSpec(memory_space=pltpu.HBM),) * 2,
+        scratch_shapes=[pltpu.VMEM((SWEEPS, systems), jnp.float32), dma((systems // ROWS + 1,))],
+        compiler_params=pltpu.CompilerParams(vmem_limit_bytes=2**20),
+        name="finish",
+    )(made, sums)
 
 
 def solution(mesh):

time: 44.8 us -> 42.5 us (0.949)
  local copies, waits for them, and re-layouts: 3.48 us -> 0 us
  Pallas kernels: 40.5 us -> 41.7 us
    unnamed x4 -> x0, local copies, waits for them, and re-layouts: 3.48 us -> none
    pallas_call x1 -> x2, Pallas kernels: 40.5 us -> 41.7 us  [the longest x1 40.4 us: body(): pl.pallas_call(functools.partial(kernel, (ny, nz, cells)), out_shape=(out...]
where the time goes in v5:
time: 42.5 us; the launch traced here: 42.4 us
  Pallas kernels  41.7 us (98%)
  between operations  0.64 us (2%)
    pallas_call x1, Pallas kernels, body(): pl.pallas_call(functools.partial(kernel, (ny, nz, cells)), out_shape=(out...  40.4 us
    pallas_call x1, Pallas kernels, body(): pl.pallas_call(functools.partial(finish, mean_count), out_shape=(out, jax...  1.36 us

profile of v5, /device:TPU:1, one launch (start us, length us, event | category | flops | bytes accessed | tf_op | source)
XLA Modules:
  0.0 42.4 jit_solution(5344698292481053595)
XLA Ops:
  0.6 40.4 %sdc.1 = (f32[1,1,32,16384]{3,2,1,0:T(8,128)S(1)}, f32[8,128]{1,0:T(8,128)S(1)}) custom-call(f32[1,32,16384]{2,1,0:T(8,128)} %ss_ref.1, f32[32,16384]{1,0:T(8,128)} %cp_ref.1), custom_call_target="tpu_custom_call" | custom-call | tf_op jit(solution)/shard_map/sdc/pallas_call | solution.py:539
  41.0 1.4 %finish.1 = (f32[1,1,32,16384]{3,2,1,0:T(8,128)}, f32[3,32]{1,0:T(4,128)}) custom-call(f32[1,1,32,16384]{3,2,1,0:T(8,128)S(1)} %get-tuple-element.4.made_ref, f32[8,128]{1,0:T(8,128)S(1)} %get-tuple-element.5.sums_ref), custom_call_target="tpu_custom_call" | custom-call | tf_op jit(solution)/shard_map/finish/pallas_call | solution.py:559

commit v6 on v5

--- a/solution.py
+++ b/solution.py
@@ -87,8 +87,8 @@
 PLACES = OUT + 2 * M
 
 
-def kernel(sizes, ss_ref, cp_ref, out_ref, sums_ref, own, transit, arena, acc, st1, st2, st3,
-           wsem, csem, rsem, tsem, zsend, osend, orecv, s1s, s1r, s2s, s2r, s3s, s3r):
+def kernel(sizes, ss_ref, cp_ref, out_ref, sums_ref, own, transit, arena, acc, st1, st2,
+           wsem, csem, rsem, tsem, zsend, osend, orecv, s1s, s1r, s2s, s2r, met):
     ny, nz, cells = sizes
     half = cells // LANES // CORES
     tiles = half // TILE
@@ -194,16 +194,6 @@
             _, q, count = source(core, a)
             view = arena.at[0, :, cols(q, count)]
             pltpu.make_async_copy(view, view, rsem.at[0, a]).wait()
-
-    fetch = pltpu.make_async_copy(ss_ref.at[0, rows, :], own, wsem.at[0])
-    fetch.start()
-    local_set(0)
-
-    @pl.loop(1, sets - 1)
-    def _(a):
-        local_set(a)
-
-    local_set(sets - 1)
 
     barrier = pltpu.get_barrier_semaphore()
 
@@ -234,6 +224,16 @@
     for by in range(1, ny):
         greet(dev(lax.rem(ypos + by, ny) * nz + zpos, core), node)
     always = CORES * M - 1 + nz - 1 + ny - 1
+    fetch = pltpu.make_async_copy(ss_ref.at[0, rows, :], own, wsem.at[0])
+    fetch.start()
+    local_set(0)
+
+    @pl.loop(1, sets - 1)
+    def _(a):
+        local_set(a)
+
+    local_set(sets - 1)
+
     pl.semaphore_wait(barrier, greeted + always)
     fetch.wait()
 
@@ -248,6 +248,9 @@
     near_set(sets - 1)
     first_leg(sets - 1)
 
+    for by in range(1, ny):
+        pl.semaphore_signal(met, inc=1, device_id=(dev(lax.rem(ypos + by, ny) * nz + zpos, core), node),
+                            device_id_type=pl.DeviceIdType.MESH)
     acc[...] = jnp.zeros_like(acc)
     first = chip == 0
     second = chip == 1
@@ -463,16 +466,18 @@
         for c in flows:
             c.wait()
 
-    swap(st1, zpos, sums, [(dev(ypos * nz + lax.rem(zpos + by, nz), core), node) for by in range(1, nz)], s1s, s1r)
-    sums = (st1[0] + st1[1]) + (st1[2] + st1[3])
-    swap(st2, ypos, sums, [(dev(lax.rem(ypos + by, ny) * nz + zpos, core), node) for by in range(1, ny)], s2s, s2r)
-    sums = (st2[0] + st2[1]) + (st2[2] + st2[3])
+    pl.semaphore_wait(met, ny - 1)
+    others = [lax.rem(ypos + by, ny) * nz + lax.rem(zpos + bz, nz) for by in range(ny) for bz in range(nz) if by or bz]
+    swap(st1, chip, sums, [(dev(c, core), node) for c in others], s1s, s1r)
+    sums = st1[0]
+    for slot in range(1, chips):
+        sums = sums + st1[slot]
     me = node * CORES + core
     peers = [lax.rem(me + by, M * CORES) for by in range(1, M * CORES)]
-    swap(st3, me, sums, [(dev(chip, lax.rem(p, CORES)), lax.div(p, CORES)) for p in peers], s3s, s3r)
-    sums = st3[0]
+    swap(st2, me, sums, [(dev(chip, lax.rem(p, CORES)), lax.div(p, CORES)) for p in peers], s2s, s2r)
+    sums = st2[0]
     for slot in range(1, M * CORES):
-        sums = sums + st3[slot]
+        sums = sums + st2[slot]
     sums_ref[...] = sums
 
     def ended(flow, count):
@@ -544,12 +549,12 @@
         scratch_shapes=[
             pltpu.VMEM((ROWS, cells), jnp.float32), flat(CORES), flat(PLACES),
             pltpu.VMEM((SWEEPS, ROWS, LANES), jnp.float32),
-            pltpu.VMEM((nz, ROWS, LANES), jnp.float32),
-            pltpu.VMEM((ny, ROWS, LANES), jnp.float32),
+            pltpu.VMEM((ny * nz, ROWS, LANES), jnp.float32),
             pltpu.VMEM((M * CORES, ROWS, LANES), jnp.float32),
             dma((1,)), dma((tiles + 2,)), dma((5, tiles + 2)), dma((CORES, tiles + 2)), dma((7,)),
             dma((CORES, M)), dma((CORES, M)),
-            dma((nz,)), dma((nz,)), dma((ny,)), dma((ny,)), dma((M * CORES,)), dma((M * CORES,)),
+            dma((ny * nz,)), dma((ny * nz,)), dma((M * CORES,)), dma((M * CORES,)),
+            pltpu.SemaphoreType.REGULAR,
         ],
         compiler_params=pltpu.CompilerParams(
             collective_id=0, has_side_effects=True, vmem_limit_bytes=51 * 2**20

time: 42.5 us -> 42.2 us (level)
  the two profiles are of different devices: /device:TPU:1 before, /device:TPU:105 now
where the time goes in v6:
time: 42.2 us; the launch traced here: 42.1 us
  Pallas kernels  41.4 us (98%)
  between operations  0.64 us (2%)
    pallas_call x1, Pallas kernels, body(): pl.pallas_call(functools.partial(kernel, (ny, nz, cells)), out_shape=(out...  40.1 us
    pallas_call x1, Pallas kernels, body(): pl.pallas_call(functools.partial(finish, mean_count), out_shape=(out, jax...  1.36 us

profile of v6, /device:TPU:105, one launch (start us, length us, event | category | flops | bytes accessed | tf_op | source)
XLA Modules:
  0.0 42.1 jit_solution(2324093649550241304)
XLA Ops:
  0.6 40.1 %sdc.1 = (f32[1,1,32,16384]{3,2,1,0:T(8,128)S(1)}, f32[8,128]{1,0:T(8,128)S(1)}) custom-call(f32[1,32,16384]{2,1,0:T(8,128)} %ss_ref.1, f32[32,16384]{1,0:T(8,128)} %cp_ref.1), custom_call_target="tpu_custom_call" | custom-call | tf_op jit(solution)/shard_map/sdc/pallas_call | solution.py:544
  40.7 1.4 %finish.1 = (f32[1,1,32,16384]{3,2,1,0:T(8,128)}, f32[3,32]{1,0:T(4,128)}) custom-call(f32[1,1,32,16384]{3,2,1,0:T(8,128)S(1)} %get-tuple-element.4.made_ref, f32[8,128]{1,0:T(8,128)S(1)} %get-tuple-element.5.sums_ref), custom_call_target="tpu_custom_call" | custom-call | tf_op jit(solution)/shard_map/finish/pallas_call | solution.py:564

commit v7 on v6

--- a/solution.py
+++ b/solution.py
@@ -74,6 +74,7 @@
 
 
 LAG = 3
+MIX = 16
 AHEAD = 3
 
 
@@ -94,14 +95,19 @@
     tiles = half // TILE
     whole = cells // LANES
     chips = ny * nz
-    sets = tiles + 2
+    main_sets = tiles + 2
+    sets = main_sets + MIX // TILE + 2
+    single = (0, main_sets - 1, main_sets, sets - 1)
+    second_window = tiles + 3
+    second_pad = PAD + second_window * TILE
     tm = lax.axis_index("tm")
     node = lax.axis_index("node")
     core = lax.rem(tm, CORES)
     chip = lax.div(tm, CORES)
     zpos = lax.rem(chip, nz)
     ypos = lax.div(chip, nz)
-    rows = pl.ds(pl.multiple_of(node * ROWS, ROWS), ROWS)
+    blocks = (node, lax.rem(node + 2, M))
+    rows = [pl.ds(pl.multiple_of(b * ROWS, ROWS), ROWS) for b in blocks]
 
     middle = jnp.where(zpos == 0, chip + nz - 1, chip - 1)
     source_chip = jnp.where(zpos == nz - 1, chip - nz + 1, chip + 1)
@@ -127,53 +133,70 @@
             src, dst, send, recv, device_id=(to_tm, to_node), device_id_type=pl.DeviceIdType.MESH
         )
 
-    def source(which, a):
-        if isinstance(a, int) and a == 0:
-            return lax.rem(half * which + whole - 1, whole), PAD - 1, 1
-        count = 1 if isinstance(a, int) and a == sets - 1 else TILE
-        return lax.rem(half * which + TILE * (a - 1), whole), PAD + TILE * (a - 1), count
+    def source(which, a, part=0):
+        if isinstance(a, int):
+            part = 1 if a >= main_sets else 0
+        b = a - part * main_sets
+        j = -1 if isinstance(b, int) and b == 0 else TILE * (b - 1)
+        first_column = half * which + (half - MIX if part else 0)
+        count = 1 if isinstance(a, int) and a in single else TILE
+        return part, lax.rem(first_column + j + whole, whole), (second_pad if part else PAD) + j, count
 
     def each_set(a, what):
-        pl.when(a < sets - 1)(lambda: what(a))
-        pl.when(a == sets - 1)(lambda: what(sets - 1))
-
-    def local_set(a):
-        start, q, count = source(core, a)
-        pltpu.make_async_copy(cp_ref.at[rows, cols(start, count)], arena.at[CP, :, cols(q, count)], csem.at[a]).start()
+        pl.when(a < main_sets - 1)(lambda: what(a))
+        pl.when(a == main_sets - 1)(lambda: what(main_sets - 1))
+
+    def in_turn(what):
+        what(0)
+        pl.loop(1, main_sets - 1)(lambda a: what(a))
+        what(main_sets - 1)
+        what(main_sets)
+        pl.loop(main_sets + 1, sets - 1)(lambda a: what(a, 1))
+        what(sets - 1)
+
+    def local_set(a, part=0):
+        part, start, q, count = source(core, a, part)
         pltpu.make_async_copy(
-            ss_ref.at[0, rows, cols(start, count)], arena.at[3 + core, :, cols(q, count)], rsem.at[3 + core, a]
+            cp_ref.at[rows[part], cols(start, count)], arena.at[CP, :, cols(q, count)], csem.at[a]
         ).start()
-
-    def near_set(a):
+        pltpu.make_async_copy(
+            ss_ref.at[0, rows[part], cols(start, count)], arena.at[3 + core, :, cols(q, count)], rsem.at[3 + core, a]
+        ).start()
+
+    def near_set(a, part=0):
         @pl.when(has_next)
         def _():
             for which in range(CORES):
-                start, q, count = source(which, a)
-                remote(own.at[:, cols(start, count)], arena.at[1 + core, :, cols(q, count)],
+                p, start, q, count = source(which, a, part)
+                remote(own.at[p, :, cols(start, count)], arena.at[1 + core, :, cols(q, count)],
                        zsend.at[which], rsem.at[1 + core, a], dev(chip + 1, which), node).start()
 
-        start, q, count = source(1 - core, a)
-        remote(own.at[:, cols(start, count)], arena.at[3 + core, :, cols(q, count)],
+        p, start, q, count = source(1 - core, a, part)
+        remote(own.at[p, :, cols(start, count)], arena.at[3 + core, :, cols(q, count)],
                zsend.at[4], rsem.at[3 + core, a], dev(chip, 1 - core), node).start()
 
-    def first_leg(a):
+    def first_leg(a, part=0):
         @pl.when(far_source)
         def _():
             for which in range(CORES):
-                start, q, count = source(which, a)
-                remote(own.at[:, cols(start, count)], transit.at[which, :, cols(q, count)],
+                p, start, q, count = source(which, a, part)
+                remote(own.at[p, :, cols(start, count)], transit.at[which, :, cols(q, count)],
                        zsend.at[2 + which], tsem.at[which, a], dev(middle, 0), node).start()
 
-    def second_leg(a):
+    def near_and_leg(a, part=0):
+        near_set(a, part)
+        first_leg(a, part)
+
+    def second_leg(a, part=0):
         for which in range(CORES):
-            _, q, count = source(which, a)
+            _, _, q, count = source(which, a, part)
             view = transit.at[which, :, cols(q, count)]
             pltpu.make_async_copy(view, view, tsem.at[which, a]).wait()
             remote(view, arena.at[0, :, cols(q, count)],
                    zsend.at[5 + which], rsem.at[0, a], dev(target, which), node).start()
 
-    def wait_set(a):
-        _, q, count = source(core, a)
+    def wait_set(a, part=0):
+        _, _, q, count = source(core, a, part)
         pltpu.make_async_copy(arena.at[CP, :, cols(q, count)], arena.at[CP, :, cols(q, count)], csem.at[a]).wait()
 
         def arrived(n):
@@ -188,10 +211,10 @@
             arrived(1)
             arrived(2)
 
-    def wait_far_set(a):
+    def wait_far_set(a, part=0):
         @pl.when(far_target)
         def _():
-            _, q, count = source(core, a)
+            _, _, q, count = source(core, a, part)
             view = arena.at[0, :, cols(q, count)]
             pltpu.make_async_copy(view, view, rsem.at[0, a]).wait()
 
@@ -224,29 +247,15 @@
     for by in range(1, ny):
         greet(dev(lax.rem(ypos + by, ny) * nz + zpos, core), node)
     always = CORES * M - 1 + nz - 1 + ny - 1
-    fetch = pltpu.make_async_copy(ss_ref.at[0, rows, :], own, wsem.at[0])
-    fetch.start()
-    local_set(0)
-
-    @pl.loop(1, sets - 1)
-    def _(a):
-        local_set(a)
-
-    local_set(sets - 1)
+    fetches = [pltpu.make_async_copy(ss_ref.at[0, rows[p], :], own.at[p], wsem.at[p]) for p in range(2)]
+    for fetch in fetches:
+        fetch.start()
+    in_turn(local_set)
 
     pl.semaphore_wait(barrier, greeted + always)
-    fetch.wait()
-
-    near_set(0)
-    first_leg(0)
-
-    @pl.loop(1, sets - 1)
-    def _(a):
-        near_set(a)
-        first_leg(a)
-
-    near_set(sets - 1)
-    first_leg(sets - 1)
+    for fetch in fetches:
+        fetch.wait()
+    in_turn(near_and_leg)
 
     for by in range(1, ny):
         pl.semaphore_signal(met, inc=1, device_id=(dev(lax.rem(ypos + by, ny) * nz + zpos, core), node),
@@ -299,7 +308,7 @@
             whole_tile = part if whole_tile is None else whole_tile + part
         acc[k] += whole_tile
 
-    def start_sweep(v, first_col, q, slices):
+    def start_sweep(v, first_col, q, slices, counted):
         here = cols(q, SUB)
         c = load(v, CP, q)
         if 1 in slices:
@@ -332,12 +341,12 @@
                     v[E1, :, here] = new
                 else:
                     keep(v, U1 + ((n - 2) * M + m) * 3, q, new)
-                if n >= 3:
+                if n >= 3 and counted:
                     total = defect * defect if total is None else total + defect * defect
         if total is not None:
             add_up(0, first_col + q, total)
 
-    def later_sweep(v, first_col, k, q, slices):
+    def later_sweep(v, first_col, k, q, slices, counted):
         here = cols(q, SUB)
         parts = (load(v, CP, q), load(v, CL, q), load(v, CS, q))
         total = None
@@ -376,7 +385,7 @@
                     keep(v, U2 + ((n - 3) * M + m) * 3, q, new)
                 else:
                     v[OUT + (n - 3) * M + m, :, here] = new
-                if n >= 3:
+                if n >= 3 and counted:
                     total = defect * defect if total is None else total + defect * defect
         if total is not None:
             add_up(k, first_col + q, total)
@@ -384,46 +393,54 @@
     def window(step):
         return arena.at[:, :, cols(step * TILE, TILE + 6)], step * TILE
 
-    def main_part(step):
+    def main_part(step, counted=True):
         v, at = window(step)
         for g in range(0, TILE, SUB):
-            start_sweep(v, at, 3 + g, (4, 3, 2))
+            start_sweep(v, at, 3 + g, (4, 3, 2), counted)
         for g in range(0, TILE, SUB):
-            later_sweep(v, at, 1, 2 + g, (4, 3))
+            later_sweep(v, at, 1, 2 + g, (4, 3), counted)
         for g in range(0, TILE, SUB):
-            later_sweep(v, at, 2, 1 + g, (4,))
-
-    def lagging_part(step):
+            later_sweep(v, at, 2, 1 + g, (4,), counted)
+
+    def lagging_part(step, counted=True):
         v, at = window(step)
         for g in range(0, TILE, SUB):
-            start_sweep(v, at, 3 + g, (1,))
+            start_sweep(v, at, 3 + g, (1,), counted)
         for g in range(0, TILE, SUB):
-            later_sweep(v, at, 1, 2 + g, (2,))
+            later_sweep(v, at, 1, 2 + g, (2,), counted)
         for g in range(0, TILE, SUB):
-            later_sweep(v, at, 2, 1 + g, (3,))
-
-    def send_out(which, i):
-        place = cols(core * half + TILE * i, TILE)
-        for away in range(M):
+            later_sweep(v, at, 2, 1 + g, (3,), counted)
+
+    step_of = (1, M - 1)
+
+    def send_out(which, i, part=0):
+        place = cols(core * half + TILE * i + (half - MIX if part else 0), TILE)
+        dst = out_ref.at[0, 0, rows[part], place]
+
+        def out(away):
             to_node = lax.rem(node + away, M)
-            src = arena.at[OUT + which * M + to_node, :, cols(PAD + TILE * i, TILE)]
-            dst = out_ref.at[0, 0, rows, place]
-            out = remote(src, dst, osend.at[which, away], orecv.at[core, away], dev(chip, which), to_node)
+            src = arena.at[OUT + which * M + to_node, :, cols((second_pad if part else PAD) + TILE * i, TILE)]
+            to = remote(src, dst, osend.at[which, away], orecv.at[core, away], dev(chip, which), to_node)
             if away:
-                out.start()
+                to.start()
             else:
-                pl.when(core != which)(out.start)
+                pl.when(core != which)(to.start)
                 pl.when(core == which)(pltpu.make_async_copy(src, dst, osend.at[which, 0]).start)
+
+        out(step_of[which])
+        if not part:
+            @pl.when(i < (half - MIX) // TILE)
+            def _():
+                out(2)
+                out(M - step_of[which])
+        out(0)
 
     wait_set(0)
 
     @pl.when(far_middle)
     def _():
         second_leg(0)
-
-        @pl.loop(1, AHEAD)
-        def _(a):
-            second_leg(a)
+        pl.loop(1, AHEAD)(lambda a: second_leg(a))
 
     wait_far_set(0)
 
@@ -431,7 +448,16 @@
     def _(step):
         @pl.when(far_middle)
         def _():
-            each_set(step + AHEAD, second_leg)
+            a = step + AHEAD
+            each_set(a, second_leg)
+
+            @pl.when(a == main_sets)
+            def _():
+                second_leg(main_sets)
+
+            @pl.when(jnp.logical_and(a > main_sets, a < sets - 1))
+            def _():
+                second_leg(a, 1)
 
         @pl.when(step <= tiles)
         def _():
@@ -446,6 +472,11 @@
             each_set(i + 2, wait_far_set)
             lagging_part(step - LAG)
             pl.when(i >= 0)(lambda: send_out(0, i))
+
+    @pl.when(far_middle)
+    def _():
+        pl.loop(tiles + 1 + LAG + AHEAD, sets - 1)(lambda a: second_leg(a, 1))
+        second_leg(sets - 1)
 
     row = lax.broadcasted_iota(jnp.int32, (ROWS, LANES), 0)
     column = lax.broadcasted_iota(jnp.int32, (ROWS, LANES), 1)
@@ -463,55 +494,84 @@
         ]
         for c in flows:
             c.start()
-        for c in flows:
-            c.wait()
+        return flows
 
     pl.semaphore_wait(met, ny - 1)
     others = [lax.rem(ypos + by, ny) * nz + lax.rem(zpos + bz, nz) for by in range(ny) for bz in range(nz) if by or bz]
-    swap(st1, chip, sums, [(dev(c, core), node) for c in others], s1s, s1r)
+    flows = swap(st1, chip, sums, [(dev(c, core), node) for c in others], s1s, s1r)
+
+    wait_set(main_sets)
+    wait_far_set(main_sets)
+
+    @pl.loop(0, MIX // TILE + 1)
+    def _(step):
+        a = main_sets + 1 + step
+
+        def arrive(a):
+            wait_set(a, 1)
+            wait_far_set(a, 1)
+
+        pl.when(a < sets - 1)(lambda: arrive(a))
+        pl.when(a == sets - 1)(lambda: arrive(sets - 1))
+        main_part(second_window + step, False)
+        lagging_part(second_window + step, False)
+
+        @pl.when(step > 0)
+        def _():
+            send_out(1, step - 1, 1)
+            send_out(0, step - 1, 1)
+
+    for c in flows:
+        c.wait()
     sums = st1[0]
     for slot in range(1, chips):
         sums = sums + st1[slot]
     me = node * CORES + core
     peers = [lax.rem(me + by, M * CORES) for by in range(1, M * CORES)]
-    swap(st2, me, sums, [(dev(chip, lax.rem(p, CORES)), lax.div(p, CORES)) for p in peers], s2s, s2r)
+    flows = swap(st2, me, sums, [(dev(chip, lax.rem(p, CORES)), lax.div(p, CORES)) for p in peers], s2s, s2r)
+    for c in flows:
+        c.wait()
     sums = st2[0]
     for slot in range(1, M * CORES):
         sums = sums + st2[slot]
     sums_ref[...] = sums
 
     def ended(flow, count):
-        view = own.at[:, cols(0, count)]
+        view = own.at[0, :, cols(0, count)]
         pltpu.make_async_copy(view, view, zsend.at[flow]).wait()
 
-    ended(4, 2 + TILE * (sets - 2))
+    taken = half + MIX + 4
+    ended(4, taken)
 
     @pl.when(has_next)
     def _():
-        ended(0, 2 + TILE * (sets - 2))
-        ended(1, 2 + TILE * (sets - 2))
+        ended(0, taken)
+        ended(1, taken)
 
     @pl.when(far_source)
     def _():
         for which in range(CORES):
-            ended(2 + which, 2 + TILE * (sets - 2))
+            ended(2 + which, taken)
 
     @pl.when(far_middle)
     def _():
         for which in range(CORES):
-            ended(5 + which, 2 + TILE * (sets - 2))
-
-    made = arena.at[OUT, :, cols(0, half)]
-
-    def drained(sem):
-        pltpu.make_async_copy(made, made, sem).wait()
-
-    for away in range(M):
-        for which in range(CORES):
-            drained(osend.at[which, away])
-            if away:
-                drained(orecv.at[which, away])
-    drained(orecv.at[1 - core, 0])
+            ended(5 + which, taken)
+
+    def drained(sem, count):
+        view = arena.at[OUT, :, cols(0, count)]
+        pltpu.make_async_copy(view, view, sem).wait()
+
+    more, less = half + MIX, half - MIX
+    for which in range(CORES):
+        for away in range(M):
+            drained(osend.at[which, away], more if away in (0, step_of[which]) else less)
+        drained(orecv.at[which, 2], less)
+        for away in (1, M - 1):
+            up = core == 0 if away == 1 else core == 1
+            pl.when(up)(functools.partial(drained, orecv.at[which, away], more))
+            pl.when(jnp.logical_not(up))(functools.partial(drained, orecv.at[which, away], less))
+    drained(orecv.at[1 - core, 0], more)
 
 
 def finish(mean_count, made_ref, sums_ref, out_ref, log_ref, row, sem):
@@ -535,7 +595,8 @@
     ny, nz = sizes
     half = cells // LANES // CORES
     tiles = half // TILE
-    span = half + 2 * TILE + 6
+    sets = tiles + 4 + MIX // TILE
+    span = (tiles + 3) * TILE + MIX + TILE + 6
     mean_count = float(ny * nz * CORES * M * cells)
     flat = lambda *lead: pltpu.VMEM(lead + (ROWS, span * LANES), jnp.float32)
     dma = pltpu.SemaphoreType.DMA
@@ -547,11 +608,11 @@
         in_specs=[pl.BlockSpec(memory_space=pltpu.HBM)] * 2,
         out_specs=(any_spec, pl.BlockSpec(memory_space=pltpu.VMEM)),
         scratch_shapes=[
-            pltpu.VMEM((ROWS, cells), jnp.float32), flat(CORES), flat(PLACES),
+            pltpu.VMEM((2, ROWS, cells), jnp.float32), flat(CORES), flat(PLACES),
             pltpu.VMEM((SWEEPS, ROWS, LANES), jnp.float32),
             pltpu.VMEM((ny * nz, ROWS, LANES), jnp.float32),
             pltpu.VMEM((M * CORES, ROWS, LANES), jnp.float32),
-            dma((1,)), dma((tiles + 2,)), dma((5, tiles + 2)), dma((CORES, tiles + 2)), dma((7,)),
+            dma((2,)), dma((sets,)), dma((5, sets)), dma((CORES, sets)), dma((7,)),
             dma((CORES, M)), dma((CORES, M)),
             dma((ny * nz,)), dma((ny * nz,)), dma((M * CORES,)), dma((M * CORES,)),
             pltpu.SemaphoreType.REGULAR,

time: 42.2 us -> 41.3 us (0.979)
  the two profiles are of different devices: /device:TPU:105 before, /device:TPU:1 now
where the time goes in v7:
time: 41.3 us; the launch traced here: 41.1 us
  Pallas kernels  40.5 us (98%)
  between operations  0.64 us (2%)
    pallas_call x1, Pallas kernels, body(): pl.pallas_call(functools.partial(kernel, (ny, nz, cells)), out_shape=(out...  39.1 us
    pallas_call x1, Pallas kernels, body(): pl.pallas_call(functools.partial(finish, mean_count), out_shape=(out, jax...  1.36 us

profile of v7, /device:TPU:1, one launch (start us, length us, event | category | flops | bytes accessed | tf_op | source)
XLA Modules:
  0.0 41.1 jit_solution(11415125198531883387)
XLA Ops:
  0.6 39.1 %sdc.1 = (f32[1,1,32,16384]{3,2,1,0:T(8,128)S(1)}, f32[8,128]{1,0:T(8,128)S(1)}) custom-call(f32[1,32,16384]{2,1,0:T(8,128)} %ss_ref.1, f32[32,16384]{1,0:T(8,128)} %cp_ref.1), custom_call_target="tpu_custom_call" | custom-call | tf_op jit(solution)/shard_map/sdc/pallas_call | solution.py:605
  39.8 1.4 %finish.1 = (f32[1,1,32,16384]{3,2,1,0:T(8,128)}, f32[3,32]{1,0:T(4,128)}) custom-call(f32[1,1,32,16384]{3,2,1,0:T(8,128)S(1)} %get-tuple-element.4.made_ref, f32[8,128]{1,0:T(8,128)S(1)} %get-tuple-element.5.sums_ref), custom_call_target="tpu_custom_call" | custom-call | tf_op jit(solution)/shard_map/finish/pallas_call | solution.py:625
